TPU v7x, 32 devices: a 4x4x1 block of a 4x4x8 slice. The times are simulated.
32 devices in a mesh: rep: 1 (over z), ep: 4 (over y), fsdp: 8 (over x, core).
Axes of the slice: x: 4, y: 4, z: 1, core: 2. Of those that a mesh axis runs over, the one named last changes fastest.
The devices are a block of a 4x4x8 slice.
Arguments:
- x: bfloat16 [32768, 1024], P(('rep', 'ep', 'fsdp'))
- norm_w: float32 [2, 1024], replicated
- router_w: bfloat16 [2, 1024, 32], replicated
- w_gate: bfloat16 [2, 32, 1024, 512], P(None, 'ep', None, 'fsdp')
- w_up: bfloat16 [2, 32, 1024, 512], P(None, 'ep', None, 'fsdp')
- w_down: bfloat16 [2, 32, 512, 1024], P(None, 'ep', 'fsdp')
- expert_idx: int32 [2, 32768, 8], P(None, ('rep', 'ep', 'fsdp'))
Outputs:
- output: bfloat16 [32768, 1024], P(('rep', 'ep', 'fsdp'))
All inputs are finite; a program needn't handle non-finite values.
Results may differ from a plain program's by a relative error of at most 0.012267.
Values are sent between devices in bfloat16 or wider.
A program may use at most 768 MiB of HBM per device.

v0:
```python
import jax
import jax.numpy as jnp
from jax import lax
from jax.sharding import PartitionSpec as P

NORM_EPS = 1e-5


def rms_norm(x, norm_w):
    x_f32 = x.astype(jnp.float32)
    return (x_f32 * lax.rsqrt(jnp.mean(x_f32 * x_f32, axis=-1, keepdims=True) + NORM_EPS) * norm_w).astype(jnp.bfloat16)


def route_gates(normed, router_w, expert_idx):
    logits = jnp.dot(normed, router_w, preferred_element_type=jnp.float32)
    return jax.nn.softmax(jnp.take_along_axis(logits, expert_idx, axis=-1), axis=-1)


def routed_ffn(normed, gate_wts, expert_idx, w_gate, w_up, w_down):
    tok_count, top_k = expert_idx.shape
    experts = w_gate.shape[0]
    flat_ids = expert_idx.reshape(-1)
    sort_order = jnp.argsort(flat_ids, stable=True)
    tok_rows = jnp.take(normed, sort_order // top_k, axis=0)
    group_sizes = jnp.bincount(flat_ids, length=experts).astype(jnp.int32)
    gate_proj = lax.ragged_dot(tok_rows, w_gate, group_sizes, preferred_element_type=jnp.float32)
    up_proj = lax.ragged_dot(tok_rows, w_up, group_sizes, preferred_element_type=jnp.float32)
    hidden_act = (jax.nn.silu(gate_proj) * up_proj).astype(jnp.bfloat16)
    sorted_out = lax.ragged_dot(hidden_act, w_down, group_sizes, preferred_element_type=jnp.float32)
    slot_pos = jnp.zeros_like(sort_order).at[sort_order].set(jnp.arange(sort_order.shape[0], dtype=sort_order.dtype))
    slot_out = jnp.take(sorted_out, slot_pos, axis=0).reshape(tok_count, top_k, -1)
    return jnp.sum(gate_wts[:, :, None] * slot_out, axis=1)


def solution(mesh):
    tok_spec = P(("rep", "ep", "fsdp"), None)
    idx_spec = P(None, ("rep", "ep", "fsdp"), None)
    in_specs = (tok_spec, P(None, None), P(None, None, None), P(None, "ep", None, "fsdp"), P(None, "ep", None, "fsdp"), P(None, "ep", "fsdp", None), idx_spec)

    def local_program(x, norm_w, router_w, w_gate, w_up, w_down, expert_idx):
        for layer_num in range(norm_w.shape[0]):
            full_gate = lax.all_gather(lax.all_gather(w_gate[layer_num], "fsdp", axis=2, tiled=True), "ep", axis=0, tiled=True)
            full_up = lax.all_gather(lax.all_gather(w_up[layer_num], "fsdp", axis=2, tiled=True), "ep", axis=0, tiled=True)
            full_down = lax.all_gather(lax.all_gather(w_down[layer_num], "fsdp", axis=1, tiled=True), "ep", axis=0, tiled=True)
            normed = rms_norm(x, norm_w[layer_num])
            gate_wts = route_gates(normed, router_w[layer_num], expert_idx[layer_num])
            mixed = routed_ffn(normed, gate_wts, expert_idx[layer_num], full_gate, full_up, full_down)
            x = (x.astype(jnp.float32) + mixed).astype(jnp.bfloat16)
        return x

    return jax.shard_map(local_program, mesh=mesh, in_specs=in_specs, out_specs=tok_spec, check_vma=False)
```

profile of v0, /device:TPU:97, one launch (start us, length us, event | category | flops | bytes accessed | tf_op | source)
XLA Modules:
  0.0 2214.3 jit_solution(7596818110033011608)
XLA Ops:
  20.7 40.6 %all-gather.25.cloned.1.call-done = bf16[1,8,1024,512]{2,1,0,3:T(8,128)(2,1)} async-done(((bf16[1,8,1024,64]{2,1,0,3:T(8,128)(2,1)}), bf16[1,8,1024,512]{2,1,0,3:T(8,128)(2,1)}) %all-gather.25.cloned.1.call-update) | async-done | bytes 8388624 | tf_op jit(solution)/shard_map/all_gather | solution.py:42
  74.0 36.3 %all-gather.29.cloned.1.call-done = bf16[1,8,1024,512]{2,1,0,3:T(8,128)(2,1)} async-done(((bf16[1,8,1024,64]{2,1,0,3:T(8,128)(2,1)}), bf16[1,8,1024,512]{2,1,0,3:T(8,128)(2,1)}) %all-gather.29.cloned.1.call-update) | async-done | bytes 8388624 | tf_op jit(solution)/shard_map/all_gather | solution.py:43
  122.8 36.3 %all-gather.33.cloned.1.call-done = bf16[1,8,512,1024]{3,2,0,1:T(8,128)(2,1)} async-done(((bf16[1,8,64,1024]{3,2,0,1:T(8,128)(2,1)}), bf16[1,8,512,1024]{3,2,0,1:T(8,128)(2,1)}) %all-gather.33.cloned.1.call-update) | async-done | bytes 8388624 | tf_op jit(solution)/shard_map/all_gather | solution.py:44
  159.2 48.6 %all-gather.37.cloned.1.call-done = bf16[1,8,1024,512]{2,1,0,3:T(8,128)(2,1)} async-done(((bf16[1,8,1024,64]{2,1,0,3:T(8,128)(2,1)}), bf16[1,8,1024,512]{2,1,0,3:T(8,128)(2,1)}) %all-gather.37.cloned.1.call-update) | async-done | bytes 8388624 | tf_op jit(solution)/shard_map/all_gather | solution.py:42
  220.5 35.9 %all-gather.41.cloned.1.call-done = bf16[1,8,1024,512]{2,1,0,3:T(8,128)(2,1)} async-done(((bf16[1,8,1024,64]{2,1,0,3:T(8,128)(2,1)}), bf16[1,8,1024,512]{2,1,0,3:T(8,128)(2,1)}) %all-gather.41.cloned.1.call-update) | async-done | bytes 8388624 | tf_op jit(solution)/shard_map/all_gather | solution.py:43
  269.0 36.0 %all-gather.45.cloned.1.call-done = bf16[1,8,512,1024]{3,2,0,1:T(8,128)(2,1)} async-done(((bf16[1,8,64,1024]{3,2,0,1:T(8,128)(2,1)}), bf16[1,8,512,1024]{3,2,0,1:T(8,128)(2,1)}) %all-gather.45.cloned.1.call-update) | async-done | bytes 8388624 | tf_op jit(solution)/shard_map/all_gather | solution.py:44
  306.6 57.5 %scatter_custom_fusion = s32[32]{0:T(128)} fusion(s32[8192]{0:T(1024)S(1)} %reshape.119, s32[8192]{0:T(1024)S(1)} %broadcast.120, s32[]{:T(128)} %constant.71.clone.1), kind=kCustom, calls=%fused_computation.91 | custom fusion | flops 8192 | bytes 132 | tf_op jit(solution)/shard_map/scatter-add | solution.py:25
  378.1 35.4 %gather_fusion.1 = bf16[8192,1024]{1,0:T(8,128)(2,1)} fusion(bf16[1024,1024]{1,0:T(8,128)(2,1)S(1)} %fusion.4, s32[8192]{0:T(1024)S(1)} %get-tuple-element.49), kind=kCustom, calls=%fused_computation.1.clone | custom fusion | bytes 33587200 | tf_op jit(solution)/shard_map/jit(_take)/gather | solution.py:24
  414.3 65.5 %gather_fusion = f32[8192]{0:T(1024)S(1)} fusion(f32[1024,32]{0,1:T(8,128)S(1)} %fusion.16, s32[8192]{0:T(1024)S(1)} %reshape.180), kind=kCustom, calls=%fused_computation.clone | custom fusion | bytes 131072 | tf_op jit(solution)/shard_map/jit(take_along_axis)/gather | solution.py:16
  481.9 57.8 %scatter_custom_fusion.2 = s32[32]{0:T(128)} fusion(s32[8192]{0:T(1024)S(1)} %reshape.135, s32[8192]{0:T(1024)} %copy-done.21, s32[]{:T(128)} %constant.71.clone.1), kind=kCustom, calls=%fused_computation.89 | custom fusion | flops 8192 | bytes 640 | tf_op jit(solution)/shard_map/scatter-add | solution.py:25
  542.3 31.2 %scatter_custom_fusion.1 = s32[8192]{0:T(1024)S(1)} fusion(s32[8192]{0:T(1024)} %get-tuple-element.48, s32[8192]{0:T(1024)S(1)} %iota.14, s32[]{:T(128)} %constant.71.clone.1), kind=kCustom, calls=%fused_computation.85 | custom fusion | bytes 33280 | tf_op jit(solution)/shard_map/scatter | solution.py:30
  580.9 30.5 %scatter_custom_fusion.3 = s32[8192]{0:T(1024)S(1)} fusion(s32[8192]{0:T(1024)S(1)} %get-tuple-element.46, s32[8192]{0:T(1024)S(1)} %iota.16, s32[]{:T(128)} %constant.71.clone.1), kind=kCustom, calls=%fused_computation.83 | custom fusion | bytes 32772 | tf_op jit(solution)/shard_map/scatter | solution.py:30
  615.7 14.2 broadcast_select_fusion.1
  629.9 59.5 %ragged-dot-none.5 = f32[8192,512]{1,0:T(8,128)} custom-call(s32[1]{0:T(128)} %get-tuple-element.24, s32[33]{0:T(128)} %get-tuple-element.25, s32[63]{0:T(128)} %get-tuple-element.26, s32[63]{0:T(128)} %get-tuple-element.27, s32[1]{0:T(128)} %get-tuple-element.24, bf16[8192,1024]{1,0:T(8,128)(2,1)} %broadcast_select_fusion.1, bf16[32,1024,512]{2,1,0:T(8,128)(2,1)} %bitcast.64), custom_call_target="tpu_custom_call" | custom-call | flops 8589934592 | bytes 67108992 | tf_op jit(solution)/shard_map/ragged_dot_general/ragged-dot-none
  689.4 202.9 %all-gather.31.cloned.1.call-done = bf16[1,32,1024,512]{3,2,0,1:T(8,128)(2,1)} async-done(((bf16[1,8,1024,512]{3,2,0,1:T(8,128)(2,1)}), bf16[1,32,1024,512]{3,2,0,1:T(8,128)(2,1)}) %all-gather.31.cloned.1.call-update) | async-done | bytes 33554448 | tf_op jit(solution)/shard_map/all_gather | solution.py:43
  892.3 59.4 %ragged-dot-none.4 = f32[8192,512]{1,0:T(8,128)} custom-call(s32[1]{0:T(128)} %get-tuple-element.24, s32[33]{0:T(128)} %get-tuple-element.25, s32[63]{0:T(128)} %get-tuple-element.26, s32[63]{0:T(128)} %get-tuple-element.27, s32[1]{0:T(128)} %get-tuple-element.24, bf16[8192,1024]{1,0:T(8,128)(2,1)} %broadcast_select_fusion.1, bf16[32,1024,512]{2,1,0:T(8,128)(2,1)} %bitcast.65), custom_call_target="tpu_custom_call" | custom-call | flops 8589934592 | bytes 67108992 | tf_op jit(solution)/shard_map/ragged_dot_general/ragged-dot-none
  951.7 15.1 multiply_convert_fusion.1
  966.8 219.8 %all-gather.35.cloned.1.call-done = bf16[1,32,512,1024]{3,2,0,1:T(8,128)(2,1)} async-done(((bf16[1,8,512,1024]{3,2,0,1:T(8,128)(2,1)}), bf16[1,32,512,1024]{3,2,0,1:T(8,128)(2,1)}) %all-gather.35.cloned.1.call-update) | async-done | bytes 33554448 | tf_op jit(solution)/shard_map/all_gather | solution.py:44
  1186.5 62.3 %ragged-dot-none.3 = f32[8192,1024]{1,0:T(8,128)} custom-call(s32[1]{0:T(128)} %get-tuple-element.24, s32[33]{0:T(128)} %get-tuple-element.25, s32[63]{0:T(128)} %get-tuple-element.26, s32[63]{0:T(128)} %get-tuple-element.27, s32[1]{0:T(128)} %get-tuple-element.24, bf16[8192,512]{1,0:T(8,128)(2,1)} %multiply_convert_fusion.1, bf16[32,512,1024]{2,1,0:T(8,128)(2,1)} %bitcast.61), custom_call_target="tpu_custom_call" | custom-call | flops 8589934592 | bytes 75497600 | tf_op jit(solution)/shard_map/ragged_dot_general/ragged-dot-none
  1248.9 54.1 %gather_fusion.2 = f32[8192,1024]{1,0:T(8,128)} fusion(f32[8192,1024]{1,0:T(8,128)} %ragged-dot-none.3, s32[8192]{0:T(1024)S(1)} %fusion.24), kind=kCustom, calls=%fused_computation.2.clone | custom fusion | bytes 67141632 | tf_op jit(solution)/shard_map/jit(_take)/gather | solution.py:31
  1303.0 20.1 fusion.1
  1330.0 65.5 %gather_fusion.3 = f32[8192]{0:T(1024)S(1)} fusion(f32[1024,32]{0,1:T(8,128)S(1)} %fusion.14, s32[8192]{0:T(1024)S(1)} %copy-done.1), kind=kCustom, calls=%fused_computation.3.clone | custom fusion | bytes 131072 | tf_op jit(solution)/shard_map/jit(take_along_axis)/gather | solution.py:16
  1395.9 42.5 %gather_fusion.4 = bf16[8192,1024]{1,0:T(8,128)(2,1)} fusion(bf16[1024,1024]{1,0:T(8,128)(2,1)} %copy-done, s32[8192]{0:T(1024)S(1)} %copy-done.12), kind=kCustom, calls=%fused_computation.4.clone | custom fusion | bytes 33587200 | tf_op jit(solution)/shard_map/jit(_take)/gather | solution.py:24
  1454.3 26.3 %all-gather.39.cloned.1.call-done = bf16[1,32,1024,512]{3,2,0,1:T(8,128)(2,1)} async-done(((bf16[1,8,1024,512]{3,2,0,1:T(8,128)(2,1)}), bf16[1,32,1024,512]{3,2,0,1:T(8,128)(2,1)}) %all-gather.39.cloned.1.call-update) | async-done | bytes 33554448 | tf_op jit(solution)/shard_map/all_gather | solution.py:42
  1480.7 59.9 %ragged-dot-none.2 = f32[8192,512]{1,0:T(8,128)} custom-call(s32[1]{0:T(128)} %get-tuple-element.12, s32[33]{0:T(128)} %get-tuple-element.13, s32[63]{0:T(128)} %get-tuple-element.14, s32[63]{0:T(128)} %get-tuple-element.15, s32[1]{0:T(128)} %get-tuple-element.12, bf16[8192,1024]{1,0:T(8,128)(2,1)} %broadcast_select_fusion, bf16[32,1024,512]{2,1,0:T(8,128)(2,1)} %bitcast.62), custom_call_target="tpu_custom_call" | custom-call | flops 8589934592 | bytes 67108992 | tf_op jit(solution)/shard_map/ragged_dot_general/ragged-dot-none
  1540.6 234.4 %all-gather.43.cloned.1.call-done = bf16[1,32,1024,512]{3,2,0,1:T(8,128)(2,1)} async-done(((bf16[1,8,1024,512]{3,2,0,1:T(8,128)(2,1)}), bf16[1,32,1024,512]{3,2,0,1:T(8,128)(2,1)}) %all-gather.43.cloned.1.call-update) | async-done | bytes 33554448 | tf_op jit(solution)/shard_map/all_gather | solution.py:43
  1775.0 59.9 %ragged-dot-none.1 = f32[8192,512]{1,0:T(8,128)} custom-call(s32[1]{0:T(128)} %get-tuple-element.12, s32[33]{0:T(128)} %get-tuple-element.13, s32[63]{0:T(128)} %get-tuple-element.14, s32[63]{0:T(128)} %get-tuple-element.15, s32[1]{0:T(128)} %get-tuple-element.12, bf16[8192,1024]{1,0:T(8,128)(2,1)} %broadcast_select_fusion, bf16[32,1024,512]{2,1,0:T(8,128)(2,1)} %bitcast.63), custom_call_target="tpu_custom_call" | custom-call | flops 8589934592 | bytes 67108992 | tf_op jit(solution)/shard_map/ragged_dot_general/ragged-dot-none
  1835.0 15.0 multiply_convert_fusion
  1850.0 219.1 %all-gather.47.cloned.1.call-done = bf16[1,32,512,1024]{3,2,0,1:T(8,128)(2,1)} async-done(((bf16[1,8,512,1024]{3,2,0,1:T(8,128)(2,1)}), bf16[1,32,512,1024]{3,2,0,1:T(8,128)(2,1)}) %all-gather.47.cloned.1.call-update) | async-done | bytes 33554448 | tf_op jit(solution)/shard_map/all_gather | solution.py:44
  2069.1 63.4 %ragged-dot-none = f32[8192,1024]{1,0:T(8,128)} custom-call(s32[1]{0:T(128)} %get-tuple-element.12, s32[33]{0:T(128)} %get-tuple-element.13, s32[63]{0:T(128)} %get-tuple-element.14, s32[63]{0:T(128)} %get-tuple-element.15, s32[1]{0:T(128)} %get-tuple-element.12, bf16[8192,512]{1,0:T(8,128)(2,1)} %multiply_convert_fusion, bf16[32,512,1024]{2,1,0:T(8,128)(2,1)} %bitcast.60), custom_call_target="tpu_custom_call" | custom-call | flops 8589934592 | bytes 75497600 | tf_op jit(solution)/shard_map/ragged_dot_general/ragged-dot-none
  2132.6 54.2 %gather_fusion.5 = f32[8192,1024]{1,0:T(8,128)} fusion(f32[8192,1024]{1,0:T(8,128)} %ragged-dot-none, s32[8192]{0:T(1024)S(1)} %copy-done.13), kind=kCustom, calls=%fused_computation.5.clone | custom fusion | bytes 67141632 | tf_op jit(solution)/shard_map/jit(_take)/gather | solution.py:31
  2186.8 18.3 fusion
  (137 shorter events, 122.3 us)
Async XLA Ops:
  6.5 54.8 %all-gather.25.cloned.1.call-start = ((), (), s32[]{:S(2)}) async-start(), calls=%async_computation | async-start | bytes 9437184 | tf_op jit(solution)/shard_map/all_gather | solution.py:42
  9.9 100.3 %all-gather.29.cloned.1.call-start = ((), (), s32[]{:S(2)}) async-start(), calls=%async_computation.2 | async-start | bytes 9437184 | tf_op jit(solution)/shard_map/all_gather | solution.py:43
  13.4 145.6 %all-gather.33.cloned.1.call-start = ((), (), s32[]{:S(2)}) async-start(), calls=%async_computation.4 | async-start | bytes 9437184 | tf_op jit(solution)/shard_map/all_gather | solution.py:44
  16.6 191.1 %all-gather.37.cloned.1.call-start = ((), (), s32[]{:S(2)}) async-start(), calls=%async_computation.6 | async-start | bytes 9437184 | tf_op jit(solution)/shard_map/all_gather | solution.py:42
  18.3 238.1 %all-gather.41.cloned.1.call-start = ((), (), s32[]{:S(2)}) async-start(), calls=%async_computation.8 | async-start | bytes 9437184 | tf_op jit(solution)/shard_map/all_gather | solution.py:43
  20.0 285.1 %all-gather.45.cloned.1.call-start = ((), (), s32[]{:S(2)}) async-start(), calls=%async_computation.10 | async-start | bytes 9437184 | tf_op jit(solution)/shard_map/all_gather | solution.py:44
  20.7 609.2 %all-gather.27.cloned.1.call-start = ((), (), s32[]{:S(2)}) async-start(), calls=%async_computation.1 | async-start | bytes 41943040 | tf_op jit(solution)/shard_map/all_gather | solution.py:42
  73.9 818.4 %all-gather.31.cloned.1.call-start = ((), (), s32[]{:S(2)}) async-start(), calls=%async_computation.3 | async-start | bytes 41943040 | tf_op jit(solution)/shard_map/all_gather | solution.py:43
  122.7 1063.9 %all-gather.35.cloned.1.call-start = ((), (), s32[]{:S(2)}) async-start(), calls=%async_computation.5 | async-start | bytes 41943040 | tf_op jit(solution)/shard_map/all_gather | solution.py:44
  159.1 1321.6 %all-gather.39.cloned.1.call-start = ((), (), s32[]{:S(2)}) async-start(), calls=%async_computation.7 | async-start | bytes 41943040 | tf_op jit(solution)/shard_map/all_gather | solution.py:42
  220.4 1554.6 %all-gather.43.cloned.1.call-start = ((), (), s32[]{:S(2)}) async-start(), calls=%async_computation.9 | async-start | bytes 41943040 | tf_op jit(solution)/shard_map/all_gather | solution.py:43
  268.9 36.3 %copy-start.19 = (s32[2,1024,8]{1,2,0:T(8,128)S(1)}, s32[2,1024,8]{1,2,0:T(8,128)}, u32[]{:S(2)}) copy-start(s32[2,1024,8]{1,2,0:T(8,128)} %param.19) | copy-start | bytes 196612
  268.9 105.3 %copy-start.6 = (bf16[1024,1024]{1,0:T(8,128)(2,1)S(1)}, bf16[1024,1024]{1,0:T(8,128)(2,1)}, u32[]{:S(2)}) copy-start(bf16[1024,1024]{1,0:T(8,128)(2,1)} %param.13) | copy-start | bytes 6291460
  269.0 105.7 %copy-start.25 = (f32[2,1024]{1,0:T(2,128)S(1)}, f32[2,1024]{1,0:T(2,128)}, u32[]{:S(2)}) copy-start(f32[2,1024]{1,0:T(2,128)} %param.14) | copy-start | bytes 24580
  269.0 1800.1 %all-gather.47.cloned.1.call-start = ((), (), s32[]{:S(2)}) async-start(), calls=%async_computation.11 | async-start | bytes 41943040 | tf_op jit(solution)/shard_map/all_gather | solution.py:44
  306.0 61.0 %copy-start.4 = (s32[1,1024,8]{2,1,0:T(8,128)}, s32[1,1024,8]{2,1,0:T(8,128)S(1)}, u32[]{:S(2)}) copy-start(s32[1,1024,8]{2,1,0:T(8,128)S(1)} %copy.32) | copy-start | bytes 98308
  306.6 57.5 %copy-start.21 = (s32[8192]{0:T(1024)}, s32[8192]{0:T(1024)S(1)}, u32[]{:S(2)}) copy-start(s32[8192]{0:T(1024)S(1)} %broadcast.120) | copy-start | bytes 98308
  378.1 35.4 %copy-start.14 = (bf16[2,1024,32]{1,2,0:T(8,128)(2,1)S(1)}, bf16[2,1024,32]{1,2,0:T(8,128)(2,1)}, u32[]{:S(2)}) copy-start(bf16[2,1024,32]{1,2,0:T(8,128)(2,1)} %param.15) | copy-start | bytes 393220
  414.2 65.9 %copy-start.18 = (s32[1,1024,8]{1,2,0:T(8,128)S(1)}, s32[1,1024,8]{1,2,0:T(8,128)}, u32[]{:S(2)}) copy-start(s32[1,1024,8]{1,2,0:T(8,128)} %get-tuple-element.45) | copy-start | bytes 98308
  414.2 197.1 %copy-start.5 = (s32[1,1024,8]{2,1,0:T(8,128)S(1)}, s32[1,1024,8]{2,1,0:T(8,128)}, u32[]{:S(2)}) copy-start(s32[1,1024,8]{2,1,0:T(8,128)} %copy-done.4) | copy-start | bytes 98308
  414.3 197.7 %copy-start.17 = (s32[8192]{0:T(1024)S(1)}, s32[8192]{0:T(1024)}, u32[]{:S(2)}) copy-start(s32[8192]{0:T(1024)} %copy-done.16) | copy-start | bytes 98308
  480.3 149.5 %copy-start.2 = (s32[1,1024,8]{2,1,0:T(8,128)}, s32[1,1024,8]{2,1,0:T(8,128)S(1)}, u32[]{:S(2)}) copy-start(s32[1,1024,8]{2,1,0:T(8,128)S(1)} %copy.36) | copy-start | bytes 98308
  1248.9 54.1 %copy-start.10 = (f32[1024,8]{1,0:T(8,128)S(1)}, f32[1024,8]{1,0:T(8,128)}, u32[]{:S(2)}) copy-start(f32[1024,8]{1,0:T(8,128)} %fusion.10) | copy-start | bytes 98308
  1248.9 54.1 %copy-start.23 = (pred[8192]{0:T(1024)(128)(4,1)S(1)}, pred[8192]{0:T(1024)(128)(4,1)}, u32[]{:S(2)}) copy-start(pred[8192]{0:T(1024)(128)(4,1)} %compare_and_fusion.2) | copy-start | bytes 24580
  1303.0 20.1 copy-start.7
  1330.0 65.9 %copy-start.12 = (s32[8192]{0:T(1024)S(1)}, s32[8192]{0:T(1024)}, u32[]{:S(2)}) copy-start(s32[8192]{0:T(1024)} %get-tuple-element.47) | copy-start | bytes 98308
  1395.9 42.5 %copy-start.3 = (s32[1,1024,8]{2,1,0:T(8,128)S(1)}, s32[1,1024,8]{2,1,0:T(8,128)}, u32[]{:S(2)}) copy-start(s32[1,1024,8]{2,1,0:T(8,128)} %copy-done.2) | copy-start | bytes 98308
  1395.9 44.3 %copy-start.20 = (pred[8192]{0:T(1024)(128)(4,1)S(1)}, pred[8192]{0:T(1024)(128)(4,1)}, u32[]{:S(2)}) copy-start(pred[8192]{0:T(1024)(128)(4,1)} %compare_and_fusion.1) | copy-start | bytes 24580
  2069.1 63.5 %copy-start.13 = (s32[8192]{0:T(1024)S(1)}, s32[8192]{0:T(1024)}, u32[]{:S(2)}) copy-start(s32[8192]{0:T(1024)} %fusion.25) | copy-start | bytes 98308
  2132.5 54.2 %copy-start.11 = (f32[1024,8]{1,0:T(8,128)S(1)}, f32[1024,8]{1,0:T(8,128)}, u32[]{:S(2)}) copy-start(f32[1024,8]{1,0:T(8,128)} %fusion.12) | copy-start | bytes 98308
  2132.5 54.2 %copy-start.22 = (pred[8192]{0:T(1024)(128)(4,1)S(1)}, pred[8192]{0:T(1024)(128)(4,1)}, u32[]{:S(2)}) copy-start(pred[8192]{0:T(1024)(128)(4,1)} %compare_and_fusion) | copy-start | bytes 24580
  2186.8 18.3 copy-start.9
  (6 other events, 21.8 us)
Sparse Core Ops, SparseCore 0:
  10.1 51.2 all-gather.24
  63.0 47.1 all-gather.28
  111.8 47.1 all-gather.32
  160.5 47.1 all-gather.36
  209.2 47.1 all-gather.40
  257.9 47.1 all-gather.44
  306.7 291.3 all-gather.26
  599.6 292.6 all-gather.30
  893.8 292.6 all-gather.34
  1188.0 292.6 all-gather.38
  1482.2 292.7 all-gather.42
  1776.5 292.5 all-gather.46
where the time goes:
time: 2230 us; the launch traced here: 2210 us
  waiting for transfers between devices  1140 us (51%)
  local copies, waits for them, and re-layouts  449 us (20%)
  Pallas kernels  370 us (17%)
  other arithmetic  242 us (11%)
    all_gather x2, waiting for transfers between devices, local_program(): lax.all_gather(lax.all_gather(w_down[layer_num], 'fsdp', axis=1, tiled=Tr...  439 us
    all_gather x2, waiting for transfers between devices, local_program(): lax.all_gather(lax.all_gather(w_up[layer_num], 'fsdp', axis=2, tiled=True...  437 us
    another operation x6, Pallas kernels  365 us
    gather x6, local copies, waits for them, and re-layouts, route_gates(): jnp.take_along_axis(logits, expert_idx, axis=-1)  133 us
    scatter-add x2, other arithmetic, routed_ffn(): group_sizes = jnp.bincount(flat_ids, length=experts).astype(jnp.int32)  115 us
    gather x2, local copies, waits for them, and re-layouts, routed_ffn(): jnp.take(sorted_out, slot_pos, axis=0).reshape(tok_count, top_k, -1)  108 us
    all_gather x2, waiting for transfers between devices, local_program(): lax.all_gather(w_gate[layer_num], 'fsdp', axis=2, tiled=True)  89.2 us
    gather x2, local copies, waits for them, and re-layouts, routed_ffn(): tok_rows = jnp.take(normed, sort_order // top_k, axis=0)  77.9 us
  transfers between devices with their start and end apart: 12, of which 11 were waited for; matrix products, arithmetic and copies ran while one was open for 28% of the time, Pallas kernels for 14%

commit v1 on v0

v1 whole, which is shorter than its diff:
```python
import jax
import jax.numpy as jnp
from jax import lax
from jax.experimental import pallas as pl
from jax.experimental.pallas import tpu as pltpu
from jax.sharding import PartitionSpec as P

NORM_EPS = 1e-5
NT = (((1,), (1,)), ((), ()))


def rms_norm(x, norm_w):
    x_f32 = x.astype(jnp.float32)
    return (x_f32 * lax.rsqrt(jnp.mean(x_f32 * x_f32, axis=-1, keepdims=True) + NORM_EPS) * norm_w).astype(jnp.bfloat16)


def route_coeffs(normed, router_w, expert_idx):
    experts = router_w.shape[-1]
    logits = jnp.dot(normed, router_w, preferred_element_type=jnp.float32)
    hit = jnp.any(expert_idx[:, :, None] == jnp.arange(experts, dtype=jnp.int32), axis=1)
    top = jnp.max(jnp.where(hit, logits, -jnp.inf), axis=-1, keepdims=True)
    exps = jnp.where(hit, jnp.exp(jnp.where(hit, logits - top, 0.0)), 0.0)
    return exps / jnp.sum(exps, axis=-1, keepdims=True)


def expert_ffn(h_ref, coeff, wg_ref, wu_ref, wd_ref, act_ref, acc_ref, first):
    width, dim = wd_ref.shape
    fc, nc = min(width, 256), min(dim, 256)
    for f in range(width // fc):
        rows = pl.ds(f * fc, fc)
        u = lax.dot_general(h_ref[...], wg_ref[rows, :], NT, preferred_element_type=jnp.float32)
        v = lax.dot_general(h_ref[...], wu_ref[rows, :], NT, preferred_element_type=jnp.float32)
        act_ref[:, rows] = (jax.nn.silu(u) * v).astype(jnp.bfloat16)
    for n in range(dim // nc):
        cols = pl.ds(n * nc, nc)
        o = coeff * jnp.dot(act_ref[...], wd_ref[:, cols], preferred_element_type=jnp.float32)
        acc_ref[:, cols] = jnp.where(first, 0.0, acc_ref[:, cols]) + o


def ffn_kernel(h_ref, c_ref, w_ref, out_ref, w_flat, act_ref):
    e = pl.program_id(1)
    pieces, _, _, rows, dim = w_ref.shape
    lane = lax.broadcasted_iota(jnp.int32, c_ref.shape, 1)
    coeff = jnp.sum(jnp.where(lane == e, c_ref[...], 0.0), axis=1, keepdims=True)
    for m in range(3):
        w_flat[m] = w_ref[:, 0, m].reshape(pieces * rows, dim)
    expert_ffn(h_ref, coeff, w_flat.at[0], w_flat.at[1], w_flat.at[2], act_ref, out_ref, e == 0)


def dense_ffn(h, coeff, w):
    tokens, dim = h.shape
    pieces, experts, _, rows, _ = w.shape
    tb = min(tokens, 1024)
    return pl.pallas_call(
        ffn_kernel,
        grid=(tokens // tb, experts),
        in_specs=[
            pl.BlockSpec((tb, dim), lambda t, e: (t, 0)),
            pl.BlockSpec((tb, experts), lambda t, e: (t, 0)),
            pl.BlockSpec((pieces, 1, 3, rows, dim), lambda t, e: (0, e, 0, 0, 0)),
        ],
        out_specs=pl.BlockSpec((tb, dim), lambda t, e: (t, 0)),
        out_shape=jax.ShapeDtypeStruct((tokens, dim), jnp.float32),
        scratch_shapes=[pltpu.VMEM((3, pieces * rows, dim), jnp.bfloat16), pltpu.VMEM((tb, pieces * rows), jnp.bfloat16)],
        compiler_params=pltpu.CompilerParams(dimension_semantics=("arbitrary", "arbitrary"), vmem_limit_bytes=60 << 20),
        cost_estimate=pl.CostEstimate(
            flops=6 * tokens * experts * pieces * rows * dim, bytes_accessed=w.size * 2 * (tokens // tb), transcendentals=0
        ),
    )(h, coeff, w)


def solution(mesh):
    tok_spec = P(("rep", "ep", "fsdp"), None)
    idx_spec = P(None, ("rep", "ep", "fsdp"), None)
    in_specs = (tok_spec, P(None, None), P(None, None, None), P(None, "ep", None, "fsdp"), P(None, "ep", None, "fsdp"), P(None, "ep", "fsdp", None), idx_spec)

    def local_program(x, norm_w, router_w, w_gate, w_up, w_down, expert_idx):
        layers, experts = w_gate.shape[:2]
        packed = jnp.stack([w_gate.transpose(0, 1, 3, 2), w_up.transpose(0, 1, 3, 2), w_down], axis=2)
        gathered = [lax.all_gather(packed[l], "fsdp", axis=0) for l in range(layers)]
        for l in range(layers):
            normed = rms_norm(x, norm_w[l])
            coeff = route_coeffs(normed, router_w[l], expert_idx[l])
            h_all = lax.all_gather(normed, "ep", axis=0, tiled=True)
            c_all = lax.all_gather(coeff, "ep", axis=0, tiled=True)
            c_own = lax.dynamic_slice_in_dim(c_all, lax.axis_index("ep") * experts, experts, axis=1)
            partial = dense_ffn(h_all, c_own, gathered[l])
            mixed = lax.psum_scatter(partial, "ep", scatter_dimension=0, tiled=True)
            x = (x.astype(jnp.float32) + mixed).astype(jnp.bfloat16)
        return x

    return jax.shard_map(local_program, mesh=mesh, in_specs=in_specs, out_specs=tok_spec, check_vma=False)
```

time: 2230 us -> 977 us (0.44)
  waiting for transfers between devices: 1140 us -> 632 us
  local copies, waits for them, and re-layouts: 449 us -> 12.8 us
  other arithmetic: 242 us -> 17.7 us
  Pallas kernels: 370 us -> 236 us
  blocking collectives: 0 us -> 61.1 us
    all_gather x12 -> x4, waiting for transfers between devices: 1140 us -> 339 us  [the longest x2 209 us: local_program(): lax.all_gather(packed[l], 'fsdp', axis=0)]
    another operation x6 -> x0, Pallas kernels: 365 us -> none
    gather x10 -> x0, local copies, waits for them, and re-layouts: 319 us -> none  [the longest x6 133 us: route_gates(): jnp.take_along_axis(logits, expert_idx, axis=-1)]
    reduce_scatter x0 -> x2, waiting for transfers between devices: none -> 292 us  [local_program(): mixed = lax.psum_scatter(partial, 'ep', scatter_dimension=0, tiled=True)]
    pallas_call x0 -> x2, Pallas kernels: none -> 236 us  [dense_ffn(): pl.pallas_call(ffn_kernel, grid=(tokens // tb, experts), in_specs=[pl.Blo...]
    scatter-add x2 -> x0, other arithmetic: 115 us -> none  [routed_ffn(): group_sizes = jnp.bincount(flat_ids, length=experts).astype(jnp.int32)]
    scatter x2 -> x0, local copies, waits for them, and re-layouts: 61.6 us -> none  [routed_ffn(): jnp.zeros_like(sort_order).at[sort_order]]
    all_gather x0 -> x2, blocking collectives: none -> 61.1 us  [local_program(): c_all = lax.all_gather(coeff, 'ep', axis=0, tiled=True)]
  transfers between devices with their start and end apart: 12 -> 6, of which waited for: 11 -> 6; matrix products, arithmetic and copies ran while one was open for 28% -> 2% of each run, Pallas kernels for 14% -> 0%
where the time goes in v1:
time: 977 us
  waiting for transfers between devices  632 us (65%)
  Pallas kernels  236 us (24%)
  blocking collectives  61.1 us (6%)
  other arithmetic  17.7 us (2%)
  between operations  13.6 us (1%)
  local copies, waits for them, and re-layouts  12.8 us (1%)
    reduce_scatter x2, waiting for transfers between devices, local_program(): mixed = lax.psum_scatter(partial, 'ep', scatter_dimension=0, tiled=True)  292 us
    pallas_call x2, Pallas kernels, dense_ffn(): pl.pallas_call(ffn_kernel, grid=(tokens // tb, experts), in_specs=[pl.Blo...  236 us
    all_gather x2, waiting for transfers between devices, local_program(): lax.all_gather(packed[l], 'fsdp', axis=0)  209 us
    all_gather x2, waiting for transfers between devices, local_program(): h_all = lax.all_gather(normed, 'ep', axis=0, tiled=True)  130 us
    all_gather x2, blocking collectives, local_program(): c_all = lax.all_gather(coeff, 'ep', axis=0, tiled=True)  61.1 us
  transfers between devices with their start and end apart: 6, of which 6 were waited for; matrix products, arithmetic and copies ran while one was open for 2% of the time, Pallas kernels for 0%

profile of v1, /device:TPU:97, one launch (start us, length us, event | category | flops | bytes accessed | tf_op | source)
XLA Modules:
  0.0 976.6 jit_solution(1613608697789471855)
XLA Ops:
  6.6 0.9 fusion.22
  7.4 2.1 fusion
  9.5 1.9 fusion.2
  11.5 1.5 copy-done.5
  13.0 2.9 pad_maximum_fusion
  15.9 3.4 fusion.21
  19.4 0.7 copy-done.7
  20.1 0.3 fusion.8
  20.4 0.3 copy.22
  20.9 0.7 select_reduce_fusion.1
  21.9 0.4 fusion.11
  22.3 0.3 fusion.10
  22.6 40.7 %all_gather.19 = f32[4096,32]{1,0:T(8,128)S(1)} all-gather(f32[1024,32]{1,0:T(8,128)S(1)} %fusion.10), channel_id=1, replica_groups=mesh['rep'=1,'ep'=4,'fsdp'=8] {'ep'}, dimensions={0}, use_global_device_ids=true | all-gather | bytes 655360 | tf_op jit(solution)/shard_map/all_gather | solution.py:85
  63.4 2.0 constant_dynamic-slice_fusion.1.c_ref
  65.3 47.7 %all-gather.5.cloned.1.call-done.h_ref = bf16[4096,1024]{1,0:T(8,128)(2,1)} async-done(((bf16[1024,1024]{1,0:T(8,128)(2,1)}), bf16[4096,1024]{1,0:T(8,128)(2,1)}) %all-gather.5.cloned.1.call-update) | async-done | bytes 8388624 | tf_op jit(solution)/shard_map/all_gather | solution.py:84
  113.1 121.3 %all-gather.7.cloned.1.call-done.w_ref = bf16[8,8,3,64,1024]{4,3,2,1,0:T(8,128)(2,1)} async-done(((bf16[1,8,3,64,1024]{4,3,2,1,0:T(8,128)(2,1)}), bf16[8,8,3,64,1024]{4,3,2,1,0:T(8,128)(2,1)}) %all-gather.7.cloned.1.call-update) | async-done | bytes 25165840 | tf_op jit(solution)/shard_map/all_gather | solution.py:80
  234.3 118.0 %shard_map.73 = f32[4096,1024]{1,0:T(8,128)} custom-call(bf16[4096,1024]{1,0:T(8,128)(2,1)} %all-gather.5.cloned.1.call-done.h_ref, f32[4096,8]{1,0:T(8,128)} %constant_dynamic-slice_fusion.1.c_ref, bf16[8,8,3,64,1024]{4,3,2,1,0:T(8,128)(2,1)} %all-gather.7.cloned.1.call-done.w_ref), custom_call_target="tpu_custom_call" | custom-call | flops 103079215104 | bytes 100663296 | tf_op jit(solution)/shard_map/pallas_call | solution.py:54
  352.5 0.6 all-gather.11.cloned.1.call-update
  353.2 145.1 %reduce-scatter.3.cloned.1.call-done = f32[1024,1024]{1,0:T(8,128)} async-done(((f32[4096,1024]{1,0:T(8,128)}), f32[1024,1024]{1,0:T(8,128)}) %reduce-scatter.3.cloned.1.call-update) | async-done | bytes 4194320 | tf_op jit(solution)/shard_map/reduce_scatter | solution.py:88
  498.3 2.9 fusion.4
  501.2 1.3 copy-done.3
  502.5 1.9 fusion.6
  504.8 2.3 select_reduce_fusion
  507.4 0.4 fusion.13
  507.8 0.3 fusion.12
  508.1 20.4 %all_gather.22 = f32[4096,32]{1,0:T(8,128)S(1)} all-gather(f32[1024,32]{1,0:T(8,128)S(1)} %fusion.12), channel_id=1, replica_groups=mesh['rep'=1,'ep'=4,'fsdp'=8] {'ep'}, dimensions={0}, use_global_device_ids=true | all-gather | bytes 655360 | tf_op jit(solution)/shard_map/all_gather | solution.py:85
  528.5 1.9 constant_dynamic-slice_fusion.c_ref
  530.4 87.9 %all-gather.11.cloned.1.call-done.w_ref = bf16[8,8,3,64,1024]{4,3,2,1,0:T(8,128)(2,1)} async-done(((bf16[1,8,3,64,1024]{4,3,2,1,0:T(8,128)(2,1)}), bf16[8,8,3,64,1024]{4,3,2,1,0:T(8,128)(2,1)}) %all-gather.11.cloned.1.call-update) | async-done | bytes 25165840 | tf_op jit(solution)/shard_map/all_gather | solution.py:80
  618.4 82.5 %all-gather.9.cloned.1.call-done.h_ref = bf16[4096,1024]{1,0:T(8,128)(2,1)} async-done(((bf16[1024,1024]{1,0:T(8,128)(2,1)}), bf16[4096,1024]{1,0:T(8,128)(2,1)}) %all-gather.9.cloned.1.call-update) | async-done | bytes 8388624 | tf_op jit(solution)/shard_map/all_gather | solution.py:84
  700.9 118.0 %shard_map.74 = f32[4096,1024]{1,0:T(8,128)} custom-call(bf16[4096,1024]{1,0:T(8,128)(2,1)} %all-gather.9.cloned.1.call-done.h_ref, f32[4096,8]{1,0:T(8,128)} %constant_dynamic-slice_fusion.c_ref, bf16[8,8,3,64,1024]{4,3,2,1,0:T(8,128)(2,1)} %all-gather.11.cloned.1.call-done.w_ref), custom_call_target="tpu_custom_call" | custom-call | flops 103079215104 | bytes 100663296 | tf_op jit(solution)/shard_map/pallas_call | solution.py:54
  819.0 146.5 %reduce-scatter.5.cloned.1.call-done = f32[1024,1024]{1,0:T(8,128)} async-done(((f32[4096,1024]{1,0:T(8,128)}), f32[1024,1024]{1,0:T(8,128)}) %reduce-scatter.5.cloned.1.call-update) | async-done | bytes 4194320 | tf_op jit(solution)/shard_map/reduce_scatter | solution.py:88
  965.5 4.3 fusion.7
  (30 shorter events, 1.5 us)
Async XLA Ops:
  6.5 3.0 copy-start.1
  6.5 106.5 %all-gather.5.cloned.1.call-start = ((), (), s32[]{:S(2)}) async-start(), calls=%async_computation.2 | async-start | bytes 10485760 | tf_op jit(solution)/shard_map/all_gather | solution.py:84
  11.4 1.6 copy-start.5
  11.4 222.9 %all-gather.7.cloned.1.call-start = ((), (), s32[]{:S(2)}) async-start(), calls=%async_computation.3 | async-start | bytes 28311552 | tf_op jit(solution)/shard_map/all_gather | solution.py:80
  19.3 0.8 copy-start.7
  19.3 1.6 copy-start
  19.3 1.6 copy-start.6
  19.4 479.0 %reduce-scatter.3.cloned.1.call-start = ((), (), s32[]{:S(2)}) async-start(), calls=%async_computation.4 | async-start | bytes 20971520 | tf_op jit(solution)/shard_map/reduce_scatter | solution.py:88
  352.5 145.9 %copy-start.2 = (bf16[1024,1024]{1,0:T(8,128)(2,1)S(1)}, bf16[1024,1024]{1,0:T(8,128)(2,1)}, u32[]{:S(2)}) copy-start(bf16[1024,1024]{1,0:T(8,128)(2,1)} %param.7) | copy-start | bytes 6291460
  352.5 265.9 %all-gather.11.cloned.1.call-start = ((), (), s32[]{:S(2)}) async-start(), calls=%async_computation.6 | async-start | bytes 28311552 | tf_op jit(solution)/shard_map/all_gather | solution.py:80
  353.1 347.8 %all-gather.9.cloned.1.call-start = ((), (), s32[]{:S(2)}) async-start(), calls=%async_computation.5 | async-start | bytes 10485760 | tf_op jit(solution)/shard_map/all_gather | solution.py:84
  501.2 1.4 copy-start.3
  504.5 461.0 %reduce-scatter.5.cloned.1.call-start = ((), (), s32[]{:S(2)}) async-start(), calls=%async_computation.7 | async-start | bytes 20971520 | tf_op jit(solution)/shard_map/reduce_scatter | solution.py:88
  818.9 146.6 %copy-start.4 = (bf16[1024,1024]{1,0:T(8,128)(2,1)S(1)}, bf16[1024,1024]{1,0:T(8,128)(2,1)}, u32[]{:S(2)}) copy-start(bf16[1024,1024]{1,0:T(8,128)(2,1)} %copy-done.3) | copy-start | bytes 6291460
Sparse Core Ops, SparseCore 0:
  11.6 101.4 all-gather.4
  114.7 119.6 all-gather.6
  352.6 145.6 reduce-scatter.2
  499.8 118.5 all-gather.10
  619.8 81.0 all-gather.8
  819.1 146.3 reduce-scatter.4

commit v2 on v0

v2 whole, which is shorter than its diff:
```python
import functools

import jax
import jax.numpy as jnp
from jax import lax
from jax.experimental import pallas as pl
from jax.experimental.pallas import tpu as pltpu
from jax.sharding import PartitionSpec as P

NORM_EPS = 1e-5
NT = (((1,), (1,)), ((), ()))
MESH = pl.DeviceIdType.MESH
CHUNKS = 2


def rms_norm(x, norm_w):
    x_f32 = x.astype(jnp.float32)
    return (x_f32 * lax.rsqrt(jnp.mean(x_f32 * x_f32, axis=-1, keepdims=True) + NORM_EPS) * norm_w).astype(jnp.bfloat16)


def route_coeffs(normed, router_w, expert_idx):
    experts = router_w.shape[-1]
    logits = jnp.dot(normed, router_w, preferred_element_type=jnp.float32)
    hit = jnp.any(expert_idx[:, :, None] == jnp.arange(experts, dtype=jnp.int32), axis=1)
    top = jnp.max(jnp.where(hit, logits, -jnp.inf), axis=-1, keepdims=True)
    exps = jnp.where(hit, jnp.exp(jnp.where(hit, logits - top, 0.0)), 0.0)
    return exps / jnp.sum(exps, axis=-1, keepdims=True)


def ring_ids(n):
    me = lax.axis_index("ep")
    return me, lax.rem(me + 1, n), lax.rem(me + n - 1, n), lax.rem(me + n // 2, n)


def enter(peers):
    barrier = pltpu.get_barrier_semaphore()
    for peer in peers:
        pl.semaphore_signal(barrier, inc=1, device_id={"ep": peer}, device_id_type=MESH)
    pl.semaphore_wait(barrier, len(peers))


def send(src, dst, sems, i, peer):
    return pltpu.make_async_remote_copy(
        src_ref=src, dst_ref=dst, send_sem=sems.at[0, i], recv_sem=sems.at[1, i], device_id={"ep": peer}, device_id_type=MESH
    )


def share_kernel(n, h_ref, c_ref, h_all, c_all, sems):
    me, up, down, far = ring_ids(n)
    half = h_ref.shape[0] // 2
    lo, hi = pl.ds(0, half), pl.ds(half, half)
    enter((up, down, far))
    up_lo = send(h_ref.at[lo], h_all.at[me, lo], sems, 0, up)
    up_hi = send(h_ref.at[hi], h_all.at[me, hi], sems, 1, up)
    down_hi = send(h_ref.at[hi], h_all.at[me, hi], sems, 2, down)
    down_lo = send(h_ref.at[lo], h_all.at[me, lo], sems, 3, down)
    coeffs = [send(c_ref.at[peer], c_all.at[me], sems, 4 + i, peer) for i, peer in enumerate((up, down, far))]
    for copy in (up_lo, down_hi, up_hi, down_lo, *coeffs):
        copy.start()
    c_all[me] = c_ref[me]
    pass_up = send(h_all.at[down, lo], h_all.at[down, lo], sems, 7, up)
    pass_down = send(h_all.at[up, hi], h_all.at[up, hi], sems, 8, down)
    up_lo.wait_recv()
    pass_up.start()
    down_hi.wait_recv()
    pass_down.start()
    for copy in (up_hi, down_lo, pass_up, pass_down, *coeffs):
        copy.wait_recv()
    for copy in (up_lo, down_hi, up_hi, down_lo, pass_up, pass_down, *coeffs):
        copy.wait_send()


def share_tokens(n, normed, coeff_t, cid):
    tokens, dim = normed.shape
    experts = coeff_t.shape[0] // n
    return pl.pallas_call(
        functools.partial(share_kernel, n),
        in_specs=[pl.BlockSpec(memory_space=pl.ANY), pl.BlockSpec(memory_space=pltpu.VMEM)],
        out_specs=[pl.BlockSpec(memory_space=pl.ANY), pl.BlockSpec(memory_space=pltpu.VMEM)],
        out_shape=[jax.ShapeDtypeStruct((n, tokens, dim), jnp.bfloat16), jax.ShapeDtypeStruct((n, experts, tokens), jnp.float32)],
        scratch_shapes=[pltpu.SemaphoreType.DMA((2, 9))],
        compiler_params=pltpu.CompilerParams(collective_id=cid, has_side_effects=True),
        cost_estimate=pl.CostEstimate(flops=60 * 10**9, bytes_accessed=8 * tokens * dim, transcendentals=0),
    )(normed, coeff_t.reshape(n, experts, tokens))


def moe_kernel(n, x_ref, h_own, h_all, c_all, w_hbm, out_ref, acc, far_in, near_in, h_buf, w_buf, act, h_sem, w_sem, sems):
    me, up, down, far = ring_ids(n)
    pieces, _, experts, rows, dim = w_hbm.shape
    chunk = h_buf.shape[1]
    half = chunk // 2
    lo, hi = pl.ds(0, half), pl.ds(half, half)
    blocks = n * CHUNKS
    steps = blocks * experts
    fp, nc = max(1, min(pieces, 256 // rows)), min(dim, 256)

    def home(s):
        k = s % n
        return lax.rem(me + jnp.where(k == 0, n // 2, jnp.where(k == 1, n - 1, jnp.where(k == 2, 1, 0))), n)

    def token_rows(s):
        return pl.ds(pl.multiple_of((s // n) * chunk, chunk), chunk)

    def load_h(s):
        @pl.when(s % n == n - 1)
        def _():
            pltpu.make_async_copy(h_own.at[token_rows(s)], h_buf.at[s % 2], h_sem.at[s % 2]).start()

        @pl.when(s % n != n - 1)
        def _():
            pltpu.make_async_copy(h_all.at[home(s), token_rows(s)], h_buf.at[s % 2], h_sem.at[s % 2]).start()

    def wait_h(s):
        pltpu.make_async_copy(h_own.at[pl.ds(0, chunk)], h_buf.at[s % 2], h_sem.at[s % 2]).wait()

    def w_copies(t):
        e, slot = t % experts, t % 2
        return [pltpu.make_async_copy(w_hbm.at[:, m, e], w_buf.at[slot, m], w_sem.at[slot, m]) for m in range(3)]

    load_h(0)
    for copy in w_copies(0):
        copy.start()
    enter((up, down))

    def far_a(c):
        return send(acc.at[n * c, lo], far_in.at[0, c], sems, 6 * c, down)

    def far_b(c):
        return send(acc.at[n * c, hi], far_in.at[1, c], sems, 6 * c + 1, up)

    def near_down(c, r, i):
        return send(acc.at[n * c + 1, r], near_in.at[0, c, r], sems, 6 * c + 2 + i, down)

    def near_up(c, r, i):
        return send(acc.at[n * c + 2, r], near_in.at[1, c, r], sems, 6 * c + 4 + i, up)

    def step(t, carry):
        s, e, slot = t // experts, t % experts, t % 2

        @pl.when(t + 1 < steps)
        def _():
            for copy in w_copies(t + 1):
                copy.start()

        @pl.when(e == 0)
        def _():
            wait_h(s)

            @pl.when(s + 1 < blocks)
            def _():
                load_h(s + 1)

        for copy in w_copies(t):
            copy.wait()
        hs = s % 2
        coeffs = c_all[home(s), token_rows(s), :]
        lane = lax.broadcasted_iota(jnp.int32, coeffs.shape, 1)
        coeff = jnp.sum(jnp.where(lane == e, coeffs, 0.0), axis=1, keepdims=True)
        for f in range(pieces // fp):
            piece = pl.ds(f * fp, fp)
            u = lax.dot_general(h_buf[hs], w_buf[slot, 0, piece].reshape(fp * rows, dim), NT, preferred_element_type=jnp.float32)
            v = lax.dot_general(h_buf[hs], w_buf[slot, 1, piece].reshape(fp * rows, dim), NT, preferred_element_type=jnp.float32)
            act[:, pl.ds(f * fp * rows, fp * rows)] = (jax.nn.silu(u) * v).astype(jnp.bfloat16)
        for j in range(dim // nc):
            cols = pl.ds(j * nc, nc)
            o = coeff * jnp.dot(act[...], w_buf[slot, 2, :, :, cols].reshape(pieces * rows, nc), preferred_element_type=jnp.float32)
            acc[s, :, cols] = jnp.where(e == 0, 0.0, acc[s, :, cols]) + o

        @pl.when(e == experts - 1)
        def _():
            for c in range(CHUNKS):

                @pl.when(s == n * c)
                def _():
                    far_a(c).start()
                    far_b(c).start()

                @pl.when(s == n * c + 1)
                def _():
                    near_down(c, hi, 1).start()

                @pl.when(s == n * c + 2)
                def _():
                    near_up(c, lo, 0).start()
                    far_a(c).wait_recv()
                    acc[n * c + 1, lo] += far_in[0, c]
                    near_down(c, lo, 0).start()

                @pl.when(s == n * c + 3)
                def _():
                    far_b(c).wait_recv()
                    acc[n * c + 2, hi] += far_in[1, c]
                    near_up(c, hi, 1).start()

        return carry

    lax.fori_loop(0, steps, step, 0)

    for c in range(CHUNKS):
        for i, r in ((1, hi), (0, lo)) if c == 0 else ((0, lo), (1, hi)):
            near_down(c, r, i).wait_recv()
            near_up(c, r, i).wait_recv()
            tok = pl.ds(c * chunk + i * half, half)
            mixed = acc[n * c + 3, r] + near_in[0, c, r] + near_in[1, c, r]
            out_ref[tok, :] = (x_ref[tok, :].astype(jnp.float32) + mixed).astype(jnp.bfloat16)
    for c in range(CHUNKS):
        far_a(c).wait_send()
        far_b(c).wait_send()
        for i, r in ((0, lo), (1, hi)):
            near_down(c, r, i).wait_send()
            near_up(c, r, i).wait_send()


def moe_layer(n, x, normed, h_all, c_all, w, cid):
    tokens, dim = x.shape
    pieces, _, experts, rows, _ = w.shape
    chunk = tokens // CHUNKS
    half = chunk // 2
    any_spec, vmem_spec = pl.BlockSpec(memory_space=pl.ANY), pl.BlockSpec(memory_space=pltpu.VMEM)
    return pl.pallas_call(
        functools.partial(moe_kernel, n),
        in_specs=[vmem_spec, any_spec, any_spec, vmem_spec, any_spec],
        out_specs=vmem_spec,
        out_shape=jax.ShapeDtypeStruct((tokens, dim), jnp.bfloat16),
        scratch_shapes=[
            pltpu.VMEM((n * CHUNKS, chunk, dim), jnp.float32),
            pltpu.VMEM((2, CHUNKS, half, dim), jnp.float32),
            pltpu.VMEM((2, CHUNKS, chunk, dim), jnp.float32),
            pltpu.VMEM((2, chunk, dim), jnp.bfloat16),
            pltpu.VMEM((2, 3, pieces, rows, dim), jnp.bfloat16),
            pltpu.VMEM((chunk, pieces * rows), jnp.bfloat16),
            pltpu.SemaphoreType.DMA((2,)),
            pltpu.SemaphoreType.DMA((2, 3)),
            pltpu.SemaphoreType.DMA((2, 6 * CHUNKS)),
        ],
        compiler_params=pltpu.CompilerParams(collective_id=cid, has_side_effects=True, vmem_limit_bytes=62 << 20),
        cost_estimate=pl.CostEstimate(
            flops=6 * n * tokens * experts * pieces * rows * dim, bytes_accessed=w.size * 2 * n * CHUNKS, transcendentals=0
        ),
    )(x, normed, h_all, c_all, w)


def solution(mesh):
    n = mesh.shape["ep"]
    tok_spec = P(("rep", "ep", "fsdp"), None)
    idx_spec = P(None, ("rep", "ep", "fsdp"), None)
    in_specs = (tok_spec, P(None, None), P(None, None, None), P(None, "ep", None, "fsdp"), P(None, "ep", None, "fsdp"), P(None, "ep", "fsdp", None), idx_spec)

    def local_program(x, norm_w, router_w, w_gate, w_up, w_down, expert_idx):
        layers = w_gate.shape[0]
        packed = [jnp.stack([w_gate[l].transpose(0, 2, 1), w_up[l].transpose(0, 2, 1), w_down[l]], axis=0) for l in range(layers)]
        gathered = [lax.all_gather(packed[l], "fsdp", axis=0) for l in range(layers)]
        for l in range(layers):
            normed = rms_norm(x, norm_w[l])
            coeff = route_coeffs(normed, router_w[l], expert_idx[l])
            h_all, c_all = share_tokens(n, normed, coeff.T, 2 * l)
            x = moe_layer(n, x, normed, h_all, c_all.transpose(0, 2, 1), gathered[l], 2 * l + 1)
        return x

    return jax.shard_map(local_program, mesh=mesh, in_specs=in_specs, out_specs=tok_spec, check_vma=False)
```

time: 2230 us -> 558 us (0.25)
  waiting for transfers between devices: 1140 us -> 35.1 us
  local copies, waits for them, and re-layouts: 449 us -> 15.6 us
  other arithmetic: 242 us -> 9.58 us
  Pallas kernels: 370 us -> 481 us
    all_gather x12 -> x2, waiting for transfers between devices: 1140 us -> 35 us  [local_program(): lax.all_gather(packed[l], 'fsdp', axis=0)]
    pallas_call x0 -> x4, Pallas kernels: none -> 481 us  [the longest x2 331 us: moe_layer(): pl.pallas_call(functools.partial(moe_kernel, n), in_specs=[vmem_spec, any...]
    another operation x6 -> x0, Pallas kernels: 365 us -> none
    gather x10 -> x0, local copies, waits for them, and re-layouts: 319 us -> none  [the longest x6 133 us: route_gates(): jnp.take_along_axis(logits, expert_idx, axis=-1)]
    scatter-add x2 -> x0, other arithmetic: 115 us -> none  [routed_ffn(): group_sizes = jnp.bincount(flat_ids, length=experts).astype(jnp.int32)]
    scatter x2 -> x0, local copies, waits for them, and re-layouts: 61.6 us -> none  [routed_ffn(): jnp.zeros_like(sort_order).at[sort_order]]
    all_gather x4 -> x0, local copies, waits for them, and re-layouts: 49.9 us -> none  [the longest x2 25.1 us: local_program(): lax.all_gather(w_gate[layer_num], 'fsdp', axis=2, tiled=True)]
    reduce_sum x4 -> x2, other arithmetic: 39.1 us -> 0.1 us  [route_coeffs(): return exps / jnp.sum(exps, axis=-1, keepdims=True)]
  transfers between devices with their start and end apart: 12 -> 2, of which waited for: 11 -> 1; matrix products, arithmetic and copies ran while one was open for 28% -> 3% of each run, Pallas kernels for 14% -> 57%
where the time goes in v2:
time: 558 us; the launch traced here: 556 us
  Pallas kernels  481 us (86%)
  waiting for transfers between devices  35.1 us (6%)
  local copies, waits for them, and re-layouts  15.6 us (3%)
  between operations  13.6 us (2%)
  other arithmetic  9.58 us (2%)
    pallas_call x2, Pallas kernels, moe_layer(): pl.pallas_call(functools.partial(moe_kernel, n), in_specs=[vmem_spec, any...  331 us
    pallas_call x2, Pallas kernels, share_tokens(): pl.pallas_call(functools.partial(share_kernel, n), in_specs=[pl.BlockSpec...  150 us
    all_gather x2, waiting for transfers between devices, local_program(): lax.all_gather(packed[l], 'fsdp', axis=0)  35 us
  transfers between devices with their start and end apart: 2, of which 1 were waited for; matrix products, arithmetic and copies ran while one was open for 3% of the time, Pallas kernels for 57%

profile of v2, /device:TPU:97, one launch (start us, length us, event | category | flops | bytes accessed | tf_op | source)
XLA Modules:
  0.0 556.2 jit_solution(12672593658867506967)
XLA Ops:
  6.6 1.9 fusion.22
  8.5 0.3 copy-done.4
  8.8 0.6 copy-done.5
  9.4 0.6 slice_bitcast_fusion
  10.1 2.1 pad_maximum_fusion
  12.1 0.1 all-gather.5.cloned.1.call-update
  12.2 0.1 all-gather.7.cloned.1.call-start
  12.3 2.0 pad_maximum_fusion.1
  14.2 0.1 all-gather.7.cloned.1.call-update
  14.3 0.8 copy-done.8
  15.1 0.1 fusion.6
  15.2 0.7 copy-done
  15.9 0.5 fusion
  16.4 0.6 fusion.23
  17.0 0.5 fusion.2.h_ref.h_own
  17.5 1.3 copy-done.2
  18.8 0.7 select_reduce_fusion.3
  19.6 0.7 fusion.15.c_ref
  20.3 76.6 %shard_map.73 = (bf16[4,1024,1024]{2,1,0:T(8,128)(2,1)}, f32[4,8,1024]{2,1,0:T(8,128)}) custom-call(bf16[1024,1024]{1,0:T(8,128)(2,1)} %copy-done.2, f32[4,8,1024]{2,1,0:T(8,128)} %fusion.15.c_ref), custom_call_target="tpu_custom_call" | custom-call | flops 60000002048 | bytes 8388608 | tf_op jit(solution)/shard_map/pallas_call | solution.py:76
  96.9 2.8 copy.16
  99.8 0.1 fusion.7
  99.9 35.0 %all-gather.5.cloned.1.call-done = bf16[24,8,64,1024]{3,2,1,0:T(8,128)(2,1)} async-done(((bf16[3,8,64,1024]{3,2,1,0:T(8,128)(2,1)}), bf16[24,8,64,1024]{3,2,1,0:T(8,128)(2,1)}) %all-gather.5.cloned.1.call-update) | async-done | bytes 25165840 | tf_op jit(solution)/shard_map/all_gather | solution.py:252
  134.9 167.1 %shard_map.74.x_ref = bf16[1024,1024]{1,0:T(8,128)(2,1)} custom-call(bf16[1024,1024]{1,0:T(8,128)(2,1)} %x_ref.1, bf16[1024,1024]{1,0:T(8,128)(2,1)} %copy-done.2, bf16[4,1024,1024]{2,1,0:T(8,128)(2,1)} %get-tuple-element.9.h_all, f32[4,1024,8]{2,1,0:T(8,128)} %bitcast.74, bf16[8,3,8,64,1024]{4,3,2,1,0:T(8,128)(2,1)} %bitcast.79), custom_call_target="tpu_custom_call" | custom-call | flops 103079215104 | bytes 201326592 | tf_op jit(solution)/shard_map/pallas_call | solution.py:220
  302.1 2.2 fusion.3
  304.3 0.5 fusion.5.h_ref.h_own
  304.9 0.7 select_reduce_fusion.1
  305.7 0.1 select_reduce_fusion
  305.7 0.7 fusion.11.c_ref
  306.4 73.3 %shard_map.75 = (bf16[4,1024,1024]{2,1,0:T(8,128)(2,1)}, f32[4,8,1024]{2,1,0:T(8,128)}) custom-call(bf16[1024,1024]{1,0:T(8,128)(2,1)} %copy-done.3, f32[4,8,1024]{2,1,0:T(8,128)} %fusion.11.c_ref), custom_call_target="tpu_custom_call" | custom-call | flops 60000002048 | bytes 8388608 | tf_op jit(solution)/shard_map/pallas_call | solution.py:76
  379.7 2.8 copy.17
  382.5 163.7 %shard_map.76 = bf16[1024,1024]{1,0:T(8,128)(2,1)} custom-call(bf16[1024,1024]{1,0:T(8,128)(2,1)} %shard_map.74.x_ref, bf16[1024,1024]{1,0:T(8,128)(2,1)} %copy-done.3, bf16[4,1024,1024]{2,1,0:T(8,128)(2,1)} %get-tuple-element.11.h_all, f32[4,1024,8]{2,1,0:T(8,128)} %bitcast.75, bf16[8,3,8,64,1024]{4,3,2,1,0:T(8,128)(2,1)} %bitcast.78), custom_call_target="tpu_custom_call" | custom-call | flops 103079215104 | bytes 201326592 | tf_op jit(solution)/shard_map/pallas_call | solution.py:220
  546.2 3.1 copy.19
  (23 shorter events, 0.1 us)
Async XLA Ops:
  6.5 128.4 %all-gather.5.cloned.1.call-start = ((), (), s32[]{:S(2)}) async-start(), calls=%async_computation | async-start | bytes 28311552 | tf_op jit(solution)/shard_map/all_gather | solution.py:252
  6.6 2.2 copy-start.4
  6.6 2.9 copy-start.5
  12.2 370.3 %all-gather.7.cloned.1.call-start = ((), (), s32[]{:S(2)}) async-start(), calls=%async_computation.1 | async-start | bytes 28311552 | tf_op jit(solution)/shard_map/all_gather | solution.py:252
  14.2 0.8 copy-start.8
  14.2 1.6 copy-start
  14.2 2.1 copy-start.10
  15.9 3.0 copy-start.6
  17.5 1.3 copy-start.2
  134.9 169.4 %copy-start.9 = (f32[1,1024]{1,0:T(1,128)S(1)}, f32[1,1024]{1,0:T(1,128)}, u32[]{:S(2)}) copy-start(f32[1,1024]{1,0:T(1,128)} %get-tuple-element.21) | copy-start | bytes 12292
  302.1 2.3 copy-start.1
  302.1 2.8 copy-start.7
  304.9 1.5 copy-start.3
Sparse Core Ops, SparseCore 0:
  12.3 122.5 all-gather.4
  136.5 119.1 all-gather.6

commit v3 on v2

--- a/solution.py
+++ b/solution.py
@@ -84,6 +84,20 @@
     )(normed, coeff_t.reshape(n, experts, tokens))
 
 
+def add_expert(h_ref, w_ref, coeff, act, acc_ref, first):
+    _, pieces, rows, dim = w_ref.shape
+    fp, nc = max(1, min(pieces, 256 // rows)), min(dim, 256)
+    for f in range(pieces // fp):
+        piece = pl.ds(f * fp, fp)
+        u = lax.dot_general(h_ref[...], w_ref[0, piece].reshape(fp * rows, dim), NT, preferred_element_type=jnp.float32)
+        v = lax.dot_general(h_ref[...], w_ref[1, piece].reshape(fp * rows, dim), NT, preferred_element_type=jnp.float32)
+        act[:, pl.ds(f * fp * rows, fp * rows)] = (jax.nn.silu(u) * v).astype(jnp.bfloat16)
+    for j in range(dim // nc):
+        cols = pl.ds(j * nc, nc)
+        o = coeff * jnp.dot(act[...], w_ref[2, :, :, cols].reshape(pieces * rows, nc), preferred_element_type=jnp.float32)
+        acc_ref[:, cols] = jnp.where(first, 0.0, acc_ref[:, cols]) + o
+
+
 def moe_kernel(n, x_ref, h_own, h_all, c_all, w_hbm, out_ref, acc, far_in, near_in, h_buf, w_buf, act, h_sem, w_sem, sems):
     me, up, down, far = ring_ids(n)
     pieces, _, experts, rows, dim = w_hbm.shape
@@ -92,7 +106,6 @@
     lo, hi = pl.ds(0, half), pl.ds(half, half)
     blocks = n * CHUNKS
     steps = blocks * experts
-    fp, nc = max(1, min(pieces, 256 // rows)), min(dim, 256)
 
     def home(s):
         k = s % n
@@ -156,15 +169,7 @@
         coeffs = c_all[home(s), token_rows(s), :]
         lane = lax.broadcasted_iota(jnp.int32, coeffs.shape, 1)
         coeff = jnp.sum(jnp.where(lane == e, coeffs, 0.0), axis=1, keepdims=True)
-        for f in range(pieces // fp):
-            piece = pl.ds(f * fp, fp)
-            u = lax.dot_general(h_buf[hs], w_buf[slot, 0, piece].reshape(fp * rows, dim), NT, preferred_element_type=jnp.float32)
-            v = lax.dot_general(h_buf[hs], w_buf[slot, 1, piece].reshape(fp * rows, dim), NT, preferred_element_type=jnp.float32)
-            act[:, pl.ds(f * fp * rows, fp * rows)] = (jax.nn.silu(u) * v).astype(jnp.bfloat16)
-        for j in range(dim // nc):
-            cols = pl.ds(j * nc, nc)
-            o = coeff * jnp.dot(act[...], w_buf[slot, 2, :, :, cols].reshape(pieces * rows, nc), preferred_element_type=jnp.float32)
-            acc[s, :, cols] = jnp.where(e == 0, 0.0, acc[s, :, cols]) + o
+        add_expert(h_buf.at[hs], w_buf.at[slot], coeff, act, acc.at[s], e == 0)
 
         @pl.when(e == experts - 1)
         def _():
@@ -240,6 +245,149 @@
     )(x, normed, h_all, c_all, w)
 
 
+def pair_peer():
+    me = lax.axis_index("ep")
+    return me, me + 1 - 2 * (me % 2)
+
+
+def pair_share_kernel(n, h_ref, c_ref, h_par, c_par, sems):
+    me, peer = pair_peer()
+    enter((peer,))
+    copies = (
+        send(h_ref, h_par, sems, 0, peer),
+        send(c_ref.at[peer], c_par.at[0], sems, 1, peer),
+        send(c_ref.at[n - 1 - peer], c_par.at[1], sems, 2, peer),
+    )
+    for copy in copies:
+        copy.start()
+    for copy in copies:
+        copy.wait()
+
+
+def pair_share(n, normed, coeff_t, cid):
+    tokens, dim = normed.shape
+    experts = coeff_t.shape[0] // n
+    return pl.pallas_call(
+        functools.partial(pair_share_kernel, n),
+        in_specs=[pl.BlockSpec(memory_space=pl.ANY), pl.BlockSpec(memory_space=pltpu.VMEM)],
+        out_specs=[pl.BlockSpec(memory_space=pl.ANY), pl.BlockSpec(memory_space=pltpu.VMEM)],
+        out_shape=[jax.ShapeDtypeStruct((tokens, dim), jnp.bfloat16), jax.ShapeDtypeStruct((2, experts, tokens), jnp.float32)],
+        scratch_shapes=[pltpu.SemaphoreType.DMA((2, 3))],
+        compiler_params=pltpu.CompilerParams(collective_id=cid, has_side_effects=True),
+        cost_estimate=pl.CostEstimate(flops=40 * 10**9, bytes_accessed=8 * tokens * dim, transcendentals=0),
+    )(normed, coeff_t.reshape(n, experts, tokens))
+
+
+def pair_kernel(x_ref, h_own, h_par, c_own, c_par, wa_hbm, wb_hbm, out_ref, acc, near_in, h_buf, w_buf, act, h_sem, w_sem, sems):
+    me, peer = pair_peer()
+    pieces, _, experts, rows, dim = wa_hbm.shape
+    chunk = h_buf.shape[1]
+    blocks, both = 2 * CHUNKS, 2 * experts
+    steps = blocks * both
+
+    def token_rows(s):
+        return pl.ds(pl.multiple_of((s % CHUNKS) * chunk, chunk), chunk)
+
+    def load_h(s):
+        @pl.when(s < CHUNKS)
+        def _():
+            pltpu.make_async_copy(h_par.at[token_rows(s)], h_buf.at[s % 2], h_sem.at[s % 2]).start()
+
+        @pl.when(s >= CHUNKS)
+        def _():
+            pltpu.make_async_copy(h_own.at[token_rows(s)], h_buf.at[s % 2], h_sem.at[s % 2]).start()
+
+    def w_copies(w_hbm, t):
+        e, slot = t % experts, t % 2
+        return [pltpu.make_async_copy(w_hbm.at[:, m, e], w_buf.at[slot, m], w_sem.at[slot, m]) for m in range(3)]
+
+    def load_w(t):
+        @pl.when(t % both < experts)
+        def _():
+            for copy in w_copies(wa_hbm, t):
+                copy.start()
+
+        @pl.when(t % both >= experts)
+        def _():
+            for copy in w_copies(wb_hbm, t):
+                copy.start()
+
+    def sums(c):
+        return send(acc.at[c], near_in.at[c], sems, c, peer)
+
+    load_h(0)
+    load_w(0)
+    enter((peer,))
+
+    def step(t, carry):
+        s, e, slot = t // both, t % both, t % 2
+
+        @pl.when(t + 1 < steps)
+        def _():
+            load_w(t + 1)
+
+        @pl.when(e == 0)
+        def _():
+            pltpu.make_async_copy(h_own.at[pl.ds(0, chunk)], h_buf.at[s % 2], h_sem.at[s % 2]).wait()
+
+            @pl.when(s + 1 < blocks)
+            def _():
+                load_h(s + 1)
+
+        for copy in w_copies(wa_hbm, t):
+            copy.wait()
+        coeffs = jnp.where(s < CHUNKS, c_par[token_rows(s), :], c_own[token_rows(s), :])
+        lane = lax.broadcasted_iota(jnp.int32, coeffs.shape, 1)
+        coeff = jnp.sum(jnp.where(lane == e, coeffs, 0.0), axis=1, keepdims=True)
+        add_expert(h_buf.at[s % 2], w_buf.at[slot], coeff, act, acc.at[s], e == 0)
+
+        @pl.when(e == both - 1)
+        def _():
+            for c in range(CHUNKS):
+
+                @pl.when(s == c)
+                def _():
+                    sums(c).start()
+
+        return carry
+
+    lax.fori_loop(0, steps, step, 0)
+    for c in range(CHUNKS):
+        sums(c).wait_recv()
+        tok = pl.ds(c * chunk, chunk)
+        mixed = acc[CHUNKS + c] + near_in[c]
+        out_ref[tok, :] = (x_ref[tok, :].astype(jnp.float32) + mixed).astype(jnp.bfloat16)
+    for c in range(CHUNKS):
+        sums(c).wait_send()
+
+
+def pair_layer(x, normed, h_par, c_own, c_par, wa, wb, cid):
+    tokens, dim = x.shape
+    pieces, _, experts, rows, _ = wa.shape
+    chunk = tokens // CHUNKS
+    any_spec, vmem_spec = pl.BlockSpec(memory_space=pl.ANY), pl.BlockSpec(memory_space=pltpu.VMEM)
+    return pl.pallas_call(
+        pair_kernel,
+        in_specs=[vmem_spec, any_spec, any_spec, vmem_spec, vmem_spec, any_spec, any_spec],
+        out_specs=vmem_spec,
+        out_shape=jax.ShapeDtypeStruct((tokens, dim), jnp.bfloat16),
+        scratch_shapes=[
+            pltpu.VMEM((2 * CHUNKS, chunk, dim), jnp.float32),
+            pltpu.VMEM((CHUNKS, chunk, dim), jnp.float32),
+            pltpu.VMEM((2, chunk, dim), jnp.bfloat16),
+            pltpu.VMEM((2, 3, pieces, rows, dim), jnp.bfloat16),
+            pltpu.VMEM((chunk, pieces * rows), jnp.bfloat16),
+            pltpu.SemaphoreType.DMA((2,)),
+            pltpu.SemaphoreType.DMA((2, 3)),
+            pltpu.SemaphoreType.DMA((2, CHUNKS)),
+        ],
+        compiler_params=pltpu.CompilerParams(collective_id=cid, has_side_effects=True, vmem_limit_bytes=62 << 20),
+        cost_estimate=pl.CostEstimate(
+            flops=24 * tokens * experts * pieces * rows * dim, bytes_accessed=wa.size * 8 * CHUNKS, transcendentals=0
+        ),
+    )(x, normed, h_par, c_own, c_par, wa, wb)
+
+
 def solution(mesh):
     n = mesh.shape["ep"]
     tok_spec = P(("rep", "ep", "fsdp"), None)
@@ -249,12 +397,24 @@
     def local_program(x, norm_w, router_w, w_gate, w_up, w_down, expert_idx):
         layers = w_gate.shape[0]
         packed = [jnp.stack([w_gate[l].transpose(0, 2, 1), w_up[l].transpose(0, 2, 1), w_down[l]], axis=0) for l in range(layers)]
+        last, me = layers - 1, lax.axis_index("ep")
+        mirrored = lax.ppermute(packed[last], "ep", [(i, n - 1 - i) for i in range(n)])
         gathered = [lax.all_gather(packed[l], "fsdp", axis=0) for l in range(layers)]
         for l in range(layers):
             normed = rms_norm(x, norm_w[l])
             coeff = route_coeffs(normed, router_w[l], expert_idx[l])
-            h_all, c_all = share_tokens(n, normed, coeff.T, 2 * l)
-            x = moe_layer(n, x, normed, h_all, c_all.transpose(0, 2, 1), gathered[l], 2 * l + 1)
+            if l < last:
+                h_all, c_all = share_tokens(n, normed, coeff.T, 2 * l)
+                if l == 0:
+                    h_all, mirrored = lax.optimization_barrier((h_all, mirrored))
+                    gathered_mirror = lax.all_gather(mirrored, "fsdp", axis=0)
+                x = moe_layer(n, x, normed, h_all, c_all.transpose(0, 2, 1), gathered[l], 2 * l + 1)
+            else:
+                experts = coeff.shape[1] // n
+                h_par, c_par = pair_share(n, normed, coeff.T, 2 * l)
+                c_own = [lax.dynamic_slice_in_dim(coeff, row * experts, experts, axis=1) for row in (me, n - 1 - me)]
+                c_par = c_par.reshape(2 * experts, -1).T
+                x = pair_layer(x, normed, h_par, jnp.concatenate(c_own, axis=1), c_par, gathered[l], gathered_mirror, 2 * l + 1)
         return x
 
     return jax.shard_map(local_program, mesh=mesh, in_specs=in_specs, out_specs=tok_spec, check_vma=False)

time: 558 us -> 522 us (0.935)
  waiting for transfers between devices: 35.1 us -> 0.19 us
  Pallas kernels: 481 us -> 472 us
    pallas_call x0 -> x2, Pallas kernels: none -> 175 us  [the longest x1 126 us: pair_layer(): pl.pallas_call(pair_kernel, in_specs=[vmem_spec, any_spec, any_spec, vmem...]
    pallas_call x2 -> x1, Pallas kernels: 331 us -> 166 us  [moe_layer(): pl.pallas_call(functools.partial(moe_kernel, n), in_specs=[vmem_spec, any...]
    all_gather x2, waiting for transfers between devices: 35 us -> 0.02 us  [local_program(): lax.all_gather(packed[l], 'fsdp', axis=0)]
    pallas_call x2 -> x1, Pallas kernels: 150 us -> 131 us  [share_tokens(): pl.pallas_call(functools.partial(share_kernel, n), in_specs=[pl.BlockSpec...]
  transfers between devices with their start and end apart: 2 -> 4, of which waited for: 1 -> 0; matrix products, arithmetic and copies ran while one was open for 3% -> 3% of each run, Pallas kernels for 57% -> 67%
where the time goes in v3:
time: 522 us; the launch traced here: 520 us
  Pallas kernels  472 us (90%)
  local copies, waits for them, and re-layouts  15.9 us (3%)
  between operations  13.4 us (3%)
  other arithmetic  11.3 us (2%)
  starting transfers between devices  5.32 us (1%)
    pallas_call x1, Pallas kernels, moe_layer(): pl.pallas_call(functools.partial(moe_kernel, n), in_specs=[vmem_spec, any...  166 us
    pallas_call x1, Pallas kernels, share_tokens(): pl.pallas_call(functools.partial(share_kernel, n), in_specs=[pl.BlockSpec...  131 us
    pallas_call x1, Pallas kernels, pair_layer(): pl.pallas_call(pair_kernel, in_specs=[vmem_spec, any_spec, any_spec, vmem...  126 us
    pallas_call x1, Pallas kernels, pair_share(): pl.pallas_call(functools.partial(pair_share_kernel, n), in_specs=[pl.Bloc...  48.4 us
  transfers between devices with their start and end apart: 4, of which 0 were waited for; matrix products, arithmetic and copies ran while one was open for 3% of the time, Pallas kernels for 67%

profile of v3, /device:TPU:97, one launch (start us, length us, event | category | flops | bytes accessed | tf_op | source)
XLA Modules:
  0.0 519.7 jit_solution(15422244917007182306)
XLA Ops:
  6.6 1.9 fusion.24
  8.5 0.3 copy-done.5
  8.8 0.6 copy-done.6
  9.4 0.6 slice_bitcast_fusion
  10.1 2.0 pad_maximum_fusion.1
  12.1 0.1 all-gather.9.cloned.1.call-start
  12.2 2.0 pad_maximum_fusion
  14.3 0.1 all-gather.11.cloned.1.call-start
  14.4 1.8 copy-done
  16.1 5.2 collective-permute-start
  21.3 0.1 fusion.6
  21.5 2.1 fusion
  23.6 0.6 fusion.25
  24.2 0.5 fusion.2.h_ref.h_own
  24.8 1.3 copy-done.2
  26.1 0.7 select_reduce_fusion.2
  26.9 0.7 fusion.15.c_ref
  27.6 131.3 %shard_map.73 = (bf16[4,1024,1024]{2,1,0:T(8,128)(2,1)}, f32[4,8,1024]{2,1,0:T(8,128)}) custom-call(bf16[1024,1024]{1,0:T(8,128)(2,1)} %copy-done.2, f32[4,8,1024]{2,1,0:T(8,128)} %fusion.15.c_ref), custom_call_target="tpu_custom_call" | custom-call | flops 60000002048 | bytes 8388608 | tf_op jit(solution)/shard_map/pallas_call | solution.py:76
  159.0 0.1 all-gather.11.cloned.1.call-update
  159.1 0.8 copy-done.9
  159.9 1.9 copy.33
  161.8 0.1 fusion.7
  161.9 166.1 %shard_map.74.x_ref = bf16[1024,1024]{1,0:T(8,128)(2,1)} custom-call(bf16[1024,1024]{1,0:T(8,128)(2,1)} %x_ref.1, bf16[1024,1024]{1,0:T(8,128)(2,1)} %copy-done.2, bf16[4,1024,1024]{2,1,0:T(8,128)(2,1)} %get-tuple-element.12.h_all, f32[4,1024,8]{2,1,0:T(8,128)} %bitcast.76, bf16[8,3,8,64,1024]{4,3,2,1,0:T(8,128)(2,1)} %bitcast.82), custom_call_target="tpu_custom_call" | custom-call | flops 103079215104 | bytes 201326592 | tf_op jit(solution)/shard_map/pallas_call | solution.py:225
  328.0 2.2 fusion.3
  330.3 0.5 fusion.5.h_ref.h_own
  330.9 0.7 select_reduce_fusion
  331.8 1.0 copy.35.c_own
  332.8 0.7 fusion.11.c_ref
  333.5 48.4 %shard_map.75 = (bf16[1024,1024]{1,0:T(8,128)(2,1)}, f32[2,8,1024]{2,1,0:T(8,128)}) custom-call(bf16[1024,1024]{1,0:T(8,128)(2,1)} %copy-done.4, f32[4,8,1024]{2,1,0:T(8,128)} %fusion.11.c_ref), custom_call_target="tpu_custom_call" | custom-call | flops 40000000000 | bytes 8388608 | tf_op jit(solution)/shard_map/pallas_call | solution.py:270
  381.9 1.9 copy.34
  383.8 126.2 %shard_map.76 = bf16[1024,1024]{1,0:T(8,128)(2,1)} custom-call(bf16[1024,1024]{1,0:T(8,128)(2,1)} %shard_map.74.x_ref, bf16[1024,1024]{1,0:T(8,128)(2,1)} %copy-done.4, bf16[1024,1024]{1,0:T(8,128)(2,1)} %get-tuple-element.14.h_par, f32[1024,16]{1,0:T(8,128)} %copy.35.c_own, f32[1024,16]{1,0:T(8,128)} %bitcast.77, bf16[8,3,8,64,1024]{4,3,2,1,0:T(8,128)(2,1)} %bitcast.81, ...), custom_call_target="tpu_custom_call" | custom-call | flops 103079215104 | bytes 201326592 | tf_op jit(solution)/shard_map/pallas_call | solution.py:369
  510.1 3.1 copy.37
  (36 shorter events, 0.4 us)
Async XLA Ops:
  6.5 155.4 %all-gather.7.cloned.1.call-start = ((), (), s32[]{:S(2)}) async-start(), calls=%async_computation | async-start | bytes 28311552 | tf_op jit(solution)/shard_map/all_gather | solution.py:402
  6.6 2.2 copy-start.5
  6.6 2.9 copy-start.6
  12.1 371.7 %all-gather.9.cloned.1.call-start = ((), (), s32[]{:S(2)}) async-start(), calls=%async_computation.1 | async-start | bytes 28311552 | tf_op jit(solution)/shard_map/all_gather | solution.py:402
  12.2 9.1 %copy-start.10 = (s32[2,1024,8]{1,2,0:T(8,128)S(1)}, s32[2,1024,8]{1,2,0:T(8,128)}, u32[]{:S(2)}) copy-start(s32[2,1024,8]{1,2,0:T(8,128)} %param.13) | copy-start | bytes 196612
  14.2 1.9 copy-start
  14.2 9.4 %copy-start.12 = (f32[2,1024]{1,0:T(2,128)S(1)}, f32[2,1024]{1,0:T(2,128)}, u32[]{:S(2)}) copy-start(f32[2,1024]{1,0:T(2,128)} %param.8) | copy-start | bytes 24580
  14.3 369.5 %all-gather.11.cloned.1.call-start = ((), (), s32[]{:S(2)}) async-start(), calls=%async_computation.2 | async-start | bytes 28311552 | tf_op jit(solution)/shard_map/all_gather | solution.py:410
  16.1 8.1 %copy-start.1 = (bf16[1024,1024]{1,0:T(8,128)(2,1)S(1)}, bf16[1024,1024]{1,0:T(8,128)(2,1)}, u32[]{:S(2)}) copy-start(bf16[1024,1024]{1,0:T(8,128)(2,1)} %x_ref.1) | copy-start | bytes 6291460
  16.1 142.8 %collective-permute-start = (bf16[3,8,64,1024]{3,2,1,0:T(8,128)(2,1)S(1)}, bf16[3,8,64,1024]{3,2,1,0:T(8,128)(2,1)}, u32[]{:S(2)}, u32[]{:S(2)}) collective-permute-start(bf16[3,8,64,1024]{3,2,1,0:T(8,128)(2,1)S(1)} %copy-done), channel_id=1, source_target_pairs={{0,24},{8,16},{16,8},{24,0},{1,25},{9,17},{17,9},{25,1},{2,26},{10... | collective-permute-start | bytes 9437192 | tf_op jit(solution)/shard_map/ppermute | solution.py:401
  21.5 4.6 copy-start.7
  24.8 1.3 copy-start.2
  159.0 0.9 copy-start.9
  161.9 168.3 %copy-start.11 = (f32[1,1024]{1,0:T(1,128)S(1)}, f32[1,1024]{1,0:T(1,128)}, u32[]{:S(2)}) copy-start(f32[1,1024]{1,0:T(1,128)} %get-tuple-element.27) | copy-start | bytes 12292
  328.0 2.3 copy-start.3
  328.0 2.8 copy-start.8
  330.9 2.6 copy-start.4
Sparse Core Ops, SparseCore 0:
  12.3 122.5 all-gather.6
  136.5 119.1 all-gather.8
  257.2 119.1 all-gather.10

commit v4 on v2

--- a/solution.py
+++ b/solution.py
@@ -84,29 +84,76 @@
     )(normed, coeff_t.reshape(n, experts, tokens))
 
 
-def moe_kernel(n, x_ref, h_own, h_all, c_all, w_hbm, out_ref, acc, far_in, near_in, h_buf, w_buf, act, h_sem, w_sem, sems):
-    me, up, down, far = ring_ids(n)
+def add_expert(h_ref, get, dims, coeff, act, acc_ref, first):
+    pieces, rows, dim = dims
+    fp, nc = max(1, min(pieces, 256 // rows)), min(dim, 256)
+    every = slice(None)
+    for f in range(pieces // fp):
+        piece = pl.ds(f * fp, fp)
+        u = lax.dot_general(h_ref[...], get(0, piece, every).reshape(fp * rows, dim), NT, preferred_element_type=jnp.float32)
+        v = lax.dot_general(h_ref[...], get(1, piece, every).reshape(fp * rows, dim), NT, preferred_element_type=jnp.float32)
+        act[:, pl.ds(f * fp * rows, fp * rows)] = (jax.nn.silu(u) * v).astype(jnp.bfloat16)
+    for j in range(dim // nc):
+        cols = pl.ds(j * nc, nc)
+        o = coeff * jnp.dot(act[...], get(2, every, cols).reshape(pieces * rows, nc), preferred_element_type=jnp.float32)
+        acc_ref[:, cols] = o if first is True else jnp.where(first, 0.0, acc_ref[:, cols]) + o
+
+
+def pick(coeffs, e):
+    lane = lax.broadcasted_iota(jnp.int32, coeffs.shape, 1)
+    return jnp.sum(jnp.where(lane == e, coeffs, 0.0), axis=1, keepdims=True)
+
+
+def block_kernel(h_ref, c_ref, w_ref, out_ref, act):
+    e = pl.program_id(0)
+    pieces, _, _, rows, dim = w_ref.shape
+    add_expert(h_ref, lambda m, p, cols: w_ref[p, m, 0, :, cols], (pieces, rows, dim), pick(c_ref[...], e), act, out_ref, e == 0)
+
+
+def block_ffn(h, coeff, w):
+    tokens, dim = h.shape
+    pieces, _, experts, rows, _ = w.shape
+    return pl.pallas_call(
+        block_kernel,
+        grid=(experts,),
+        in_specs=[
+            pl.BlockSpec((tokens, dim), lambda e: (0, 0)),
+            pl.BlockSpec((tokens, experts), lambda e: (0, 0)),
+            pl.BlockSpec((pieces, 3, 1, rows, dim), lambda e: (0, 0, e, 0, 0)),
+        ],
+        out_specs=pl.BlockSpec((tokens, dim), lambda e: (0, 0)),
+        out_shape=jax.ShapeDtypeStruct((tokens, dim), jnp.float32),
+        scratch_shapes=[pltpu.VMEM((tokens, pieces * rows), jnp.bfloat16)],
+        compiler_params=pltpu.CompilerParams(dimension_semantics=("arbitrary",), vmem_limit_bytes=60 << 20),
+        cost_estimate=pl.CostEstimate(
+            flops=6 * tokens * experts * pieces * rows * dim, bytes_accessed=w.size * 2, transcendentals=0
+        ),
+    )(h, coeff, w)
+
+
+def moe_kernel(n, x_ref, h_own, h_all, c_all, w_hbm, far_hbm, out_ref, acc, far_out, far_in, near_in, h_buf, w_buf, act, h_sem, w_sem, far_sem, sems):
+    me, up, down, _ = ring_ids(n)
+    m1 = n - 1
     pieces, _, experts, rows, dim = w_hbm.shape
     chunk = h_buf.shape[1]
     half = chunk // 2
     lo, hi = pl.ds(0, half), pl.ds(half, half)
-    blocks = n * CHUNKS
+    blocks = m1 * CHUNKS
     steps = blocks * experts
-    fp, nc = max(1, min(pieces, 256 // rows)), min(dim, 256)
 
     def home(s):
-        k = s % n
-        return lax.rem(me + jnp.where(k == 0, n // 2, jnp.where(k == 1, n - 1, jnp.where(k == 2, 1, 0))), n)
+        k = s % m1
+        return lax.rem(me + jnp.where(k == 0, n - 1, jnp.where(k == 1, 1, 0)), n)
 
     def token_rows(s):
-        return pl.ds(pl.multiple_of((s // n) * chunk, chunk), chunk)
+        return pl.ds(pl.multiple_of((s // m1) * chunk, chunk), chunk)
 
     def load_h(s):
-        @pl.when(s % n == n - 1)
+        @pl.when(s % m1 == m1 - 1)
         def _():
             pltpu.make_async_copy(h_own.at[token_rows(s)], h_buf.at[s % 2], h_sem.at[s % 2]).start()
 
-        @pl.when(s % n != n - 1)
+        @pl.when(s % m1 != m1 - 1)
         def _():
             pltpu.make_async_copy(h_all.at[home(s), token_rows(s)], h_buf.at[s % 2], h_sem.at[s % 2]).start()
 
@@ -117,22 +164,30 @@
         e, slot = t % experts, t % 2
         return [pltpu.make_async_copy(w_hbm.at[:, m, e], w_buf.at[slot, m], w_sem.at[slot, m]) for m in range(3)]
 
+    far_loads = [pltpu.make_async_copy(far_hbm.at[pl.ds(c * chunk, chunk)], far_out.at[c], far_sem.at[c]) for c in range(CHUNKS)]
+    for copy in far_loads:
+        copy.start()
     load_h(0)
     for copy in w_copies(0):
         copy.start()
     enter((up, down))
 
     def far_a(c):
-        return send(acc.at[n * c, lo], far_in.at[0, c], sems, 6 * c, down)
+        return send(far_out.at[c, lo], far_in.at[0, c], sems, 6 * c, down)
 
     def far_b(c):
-        return send(acc.at[n * c, hi], far_in.at[1, c], sems, 6 * c + 1, up)
+        return send(far_out.at[c, hi], far_in.at[1, c], sems, 6 * c + 1, up)
 
     def near_down(c, r, i):
-        return send(acc.at[n * c + 1, r], near_in.at[0, c, r], sems, 6 * c + 2 + i, down)
+        return send(acc.at[m1 * c, r], near_in.at[0, c, r], sems, 6 * c + 2 + i, down)
 
     def near_up(c, r, i):
-        return send(acc.at[n * c + 2, r], near_in.at[1, c, r], sems, 6 * c + 4 + i, up)
+        return send(acc.at[m1 * c + 1, r], near_in.at[1, c, r], sems, 6 * c + 4 + i, up)
+
+    for c in range(CHUNKS):
+        far_loads[c].wait()
+        far_a(c).start()
+        far_b(c).start()
 
     def step(t, carry):
         s, e, slot = t // experts, t % experts, t % 2
@@ -153,43 +208,30 @@
         for copy in w_copies(t):
             copy.wait()
         hs = s % 2
-        coeffs = c_all[home(s), token_rows(s), :]
-        lane = lax.broadcasted_iota(jnp.int32, coeffs.shape, 1)
-        coeff = jnp.sum(jnp.where(lane == e, coeffs, 0.0), axis=1, keepdims=True)
-        for f in range(pieces // fp):
-            piece = pl.ds(f * fp, fp)
-            u = lax.dot_general(h_buf[hs], w_buf[slot, 0, piece].reshape(fp * rows, dim), NT, preferred_element_type=jnp.float32)
-            v = lax.dot_general(h_buf[hs], w_buf[slot, 1, piece].reshape(fp * rows, dim), NT, preferred_element_type=jnp.float32)
-            act[:, pl.ds(f * fp * rows, fp * rows)] = (jax.nn.silu(u) * v).astype(jnp.bfloat16)
-        for j in range(dim // nc):
-            cols = pl.ds(j * nc, nc)
-            o = coeff * jnp.dot(act[...], w_buf[slot, 2, :, :, cols].reshape(pieces * rows, nc), preferred_element_type=jnp.float32)
-            acc[s, :, cols] = jnp.where(e == 0, 0.0, acc[s, :, cols]) + o
+        add_expert(
+            h_buf.at[hs], lambda m, p, cols: w_buf[slot, m, p, :, cols], (pieces, rows, dim),
+            pick(c_all[home(s), token_rows(s), :], e), act, acc.at[s], e == 0,
+        )
 
         @pl.when(e == experts - 1)
         def _():
             for c in range(CHUNKS):
 
-                @pl.when(s == n * c)
-                def _():
-                    far_a(c).start()
-                    far_b(c).start()
-
-                @pl.when(s == n * c + 1)
+                @pl.when(s == m1 * c)
                 def _():
                     near_down(c, hi, 1).start()
 
-                @pl.when(s == n * c + 2)
+                @pl.when(s == m1 * c + 1)
                 def _():
                     near_up(c, lo, 0).start()
                     far_a(c).wait_recv()
-                    acc[n * c + 1, lo] += far_in[0, c]
+                    acc[m1 * c, lo] += far_in[0, c]
                     near_down(c, lo, 0).start()
 
-                @pl.when(s == n * c + 3)
+                @pl.when(s == m1 * c + 2)
                 def _():
                     far_b(c).wait_recv()
-                    acc[n * c + 2, hi] += far_in[1, c]
+                    acc[m1 * c + 1, hi] += far_in[1, c]
                     near_up(c, hi, 1).start()
 
         return carry
@@ -201,7 +243,7 @@
             near_down(c, r, i).wait_recv()
             near_up(c, r, i).wait_recv()
             tok = pl.ds(c * chunk + i * half, half)
-            mixed = acc[n * c + 3, r] + near_in[0, c, r] + near_in[1, c, r]
+            mixed = acc[m1 * c + 2, r] + near_in[0, c, r] + near_in[1, c, r]
             out_ref[tok, :] = (x_ref[tok, :].astype(jnp.float32) + mixed).astype(jnp.bfloat16)
     for c in range(CHUNKS):
         far_a(c).wait_send()
@@ -211,7 +253,7 @@
             near_up(c, r, i).wait_send()
 
 
-def moe_layer(n, x, normed, h_all, c_all, w, cid):
+def moe_layer(n, x, normed, h_all, c_all, w, far_part, cid):
     tokens, dim = x.shape
     pieces, _, experts, rows, _ = w.shape
     chunk = tokens // CHUNKS
@@ -219,11 +261,12 @@
     any_spec, vmem_spec = pl.BlockSpec(memory_space=pl.ANY), pl.BlockSpec(memory_space=pltpu.VMEM)
     return pl.pallas_call(
         functools.partial(moe_kernel, n),
-        in_specs=[vmem_spec, any_spec, any_spec, vmem_spec, any_spec],
+        in_specs=[vmem_spec, any_spec, any_spec, vmem_spec, any_spec, any_spec],
         out_specs=vmem_spec,
         out_shape=jax.ShapeDtypeStruct((tokens, dim), jnp.bfloat16),
         scratch_shapes=[
-            pltpu.VMEM((n * CHUNKS, chunk, dim), jnp.float32),
+            pltpu.VMEM(((n - 1) * CHUNKS, chunk, dim), jnp.float32),
+            pltpu.VMEM((CHUNKS, chunk, dim), jnp.float32),
             pltpu.VMEM((2, CHUNKS, half, dim), jnp.float32),
             pltpu.VMEM((2, CHUNKS, chunk, dim), jnp.float32),
             pltpu.VMEM((2, chunk, dim), jnp.bfloat16),
@@ -231,13 +274,232 @@
             pltpu.VMEM((chunk, pieces * rows), jnp.bfloat16),
             pltpu.SemaphoreType.DMA((2,)),
             pltpu.SemaphoreType.DMA((2, 3)),
+            pltpu.SemaphoreType.DMA((CHUNKS,)),
             pltpu.SemaphoreType.DMA((2, 6 * CHUNKS)),
         ],
         compiler_params=pltpu.CompilerParams(collective_id=cid, has_side_effects=True, vmem_limit_bytes=62 << 20),
         cost_estimate=pl.CostEstimate(
-            flops=6 * n * tokens * experts * pieces * rows * dim, bytes_accessed=w.size * 2 * n * CHUNKS, transcendentals=0
+            flops=6 * (n - 1) * tokens * experts * pieces * rows * dim, bytes_accessed=w.size * 2 * n * CHUNKS, transcendentals=0
         ),
-    )(x, normed, h_all, c_all, w)
+    )(x, normed, h_all, c_all, w, far_part)
+
+
+def pair_peer():
+    me = lax.axis_index("ep")
+    return me, me + 1 - 2 * (me % 2)
+
+
+def expert_loop(seq, sources, h_buf, w_buf, act, acc, load_h, wait_h, coeffs, h_sem, w_sem, w_hbm, done, fresh):
+    pieces, _, experts, rows, dim = w_hbm[0].shape
+    count = len(seq)
+
+    def at(q, j):
+        value = seq[0][j]
+        for i in range(1, count):
+            value = jnp.where(q >= i, seq[i][j], value)
+        return value
+
+    def w_copies(src, t):
+        e, slot = t % experts, t % 2
+        return [pltpu.make_async_copy(src.at[:, m, e], w_buf.at[slot, m], w_sem.at[slot, m]) for m in range(3)]
+
+    def load_w(t):
+        if sources == 1:
+            for copy in w_copies(w_hbm[0], t):
+                copy.start()
+            return
+        for i in range(2):
+
+            @pl.when(at(t // experts, 1) == i)
+            def _():
+                for copy in w_copies(w_hbm[i], t):
+                    copy.start()
+
+    load_w(0)
+    load_h(0)
+
+    def step(t, carry):
+        q, e, slot = t // experts, t % experts, t % 2
+
+        @pl.when(t + 1 < count * experts)
+        def _():
+            load_w(t + 1)
+
+        @pl.when(e == 0)
+        def _():
+            wait_h(q)
+
+            @pl.when(q + 1 < count)
+            def _():
+                load_h(q + 1)
+
+        for copy in w_copies(w_hbm[0], t):
+            copy.wait()
+        add_expert(
+            h_buf.at[q % 2], lambda m, p, cols: w_buf[slot, m, p, :, cols], (pieces, rows, dim),
+            pick(coeffs(q), at(q, 1) * experts + e), act, acc.at[at(q, 0)], jnp.logical_and(e == 0, fresh(q)),
+        )
+
+        @pl.when(e == experts - 1)
+        def _():
+            done(q)
+
+        return carry
+
+    lax.fori_loop(0, count * experts, step, 0)
+
+
+def pair_first_kernel(h_own, c_own, c_send, wa_hbm, h_par, c_par, part_hbm, acc, c_now, h_buf, w_buf, act, h_sem, w_sem, part_sem, sems):
+    me, peer = pair_peer()
+    chunk = h_buf.shape[1]
+    rows_of = [pl.ds(c * chunk, chunk) for c in range(CHUNKS)]
+    enter((peer,))
+    swaps = []
+    for c in range(CHUNKS):
+        swaps.append(send(c_send.at[rows_of[c]], c_par.at[rows_of[c]], sems, 2 * c, peer))
+        swaps.append(send(h_own.at[rows_of[c]], h_par.at[rows_of[c]], sems, 2 * c + 1, peer))
+    for copy in swaps:
+        copy.start()
+
+    def load_h(q):
+        for i in range(CHUNKS):
+
+            @pl.when(q == i)
+            def _():
+                pltpu.make_async_copy(h_own.at[rows_of[i]], h_buf.at[q % 2], h_sem.at[q % 2]).start()
+
+    def wait_h(q):
+        @pl.when(q == CHUNKS)
+        def _():
+            swaps[0].wait_recv()
+            swaps[1].wait_recv()
+            pltpu.make_async_copy(h_par.at[rows_of[0]], h_buf.at[q % 2], h_sem.at[q % 2]).start()
+            c_now[...] = c_par[rows_of[0], :]
+
+        for i in range(CHUNKS):
+
+            @pl.when(q == i)
+            def _():
+                c_now[...] = c_own[rows_of[i], :]
+
+        pltpu.make_async_copy(h_own.at[rows_of[0]], h_buf.at[q % 2], h_sem.at[q % 2]).wait()
+
+    def coeffs(q):
+        return c_now[...]
+
+    def part(i):
+        return pltpu.make_async_copy(acc.at[i], part_hbm.at[i], part_sem.at[i])
+
+    def done(q):
+        for i in range(CHUNKS + 1):
+
+            @pl.when(q == i)
+            def _():
+                part(i).start()
+
+    seq = [(i, 0) for i in range(CHUNKS + 1)]
+    expert_loop(seq, 1, h_buf, w_buf, act, acc, load_h, wait_h, coeffs, h_sem, w_sem, (wa_hbm,), done, lambda q: q >= 0)
+    for copy in swaps[2:]:
+        copy.wait_recv()
+    for copy in swaps:
+        copy.wait_send()
+    for i in range(CHUNKS + 1):
+        part(i).wait()
+
+
+def pair_second_kernel(x_ref, h_own, h_par, c_own, c_par, part_hbm, wa_hbm, wb_hbm, out_ref, acc, near_in, h_buf, w_buf, act, h_sem, w_sem, part_sem, sems):
+    me, peer = pair_peer()
+    chunk = h_buf.shape[1]
+    parts = [pltpu.make_async_copy(part_hbm.at[i], acc.at[i], part_sem.at[i]) for i in (2, 0, 1)]
+    for copy in parts:
+        copy.start()
+    enter((peer,))
+    seq = [(2, 1), (3, 0), (3, 1), (0, 1), (1, 1)]
+    tokens = [(h_par, c_par, 0), (h_par, c_par, 1), (h_par, c_par, 1), (h_own, c_own, 0), (h_own, c_own, 1)]
+
+    def sums(c):
+        return send(acc.at[CHUNKS + c], near_in.at[c], sems, c, peer)
+
+    def load_h(q):
+        for i, (h_ref, _, c) in enumerate(tokens):
+
+            @pl.when(q == i)
+            def _():
+                pltpu.make_async_copy(h_ref.at[pl.ds(c * chunk, chunk)], h_buf.at[q % 2], h_sem.at[q % 2]).start()
+
+    def wait_h(q):
+        pltpu.make_async_copy(h_own.at[pl.ds(0, chunk)], h_buf.at[q % 2], h_sem.at[q % 2]).wait()
+        for copy, i in zip(parts, (0, 3, 4)):
+
+            @pl.when(q == i)
+            def _():
+                copy.wait()
+
+    def coeffs(q):
+        second = jnp.logical_or(q == 4, jnp.logical_or(q == 1, q == 2))
+        rows = pl.ds(pl.multiple_of(jnp.where(second, chunk, 0), chunk), chunk)
+        return jnp.where(q < 3, c_par[rows, :], c_own[rows, :])
+
+    def done(q):
+        for i, c in ((0, 0), (2, 1)):
+
+            @pl.when(q == i)
+            def _():
+                sums(c).start()
+
+    expert_loop(seq, 2, h_buf, w_buf, act, acc, load_h, wait_h, coeffs, h_sem, w_sem, (wa_hbm, wb_hbm), done, lambda q: q == 1)
+    for c in range(CHUNKS):
+        sums(c).wait_recv()
+        tok = pl.ds(c * chunk, chunk)
+        out_ref[tok, :] = (x_ref[tok, :].astype(jnp.float32) + (acc[c] + near_in[c])).astype(jnp.bfloat16)
+    for c in range(CHUNKS):
+        sums(c).wait_send()
+
+
+def pair_layer(x, normed, c_own, c_send, wa, other_row, cid):
+    tokens, dim = x.shape
+    pieces, _, experts, rows, _ = wa.shape
+    chunk = tokens // CHUNKS
+    any_spec, vmem_spec = pl.BlockSpec(memory_space=pl.ANY), pl.BlockSpec(memory_space=pltpu.VMEM)
+    bufs = [
+        pltpu.VMEM((2, chunk, dim), jnp.bfloat16),
+        pltpu.VMEM((2, 3, pieces, rows, dim), jnp.bfloat16),
+        pltpu.VMEM((chunk, pieces * rows), jnp.bfloat16),
+        pltpu.SemaphoreType.DMA((2,)),
+        pltpu.SemaphoreType.DMA((2, 3)),
+        pltpu.SemaphoreType.DMA((CHUNKS + 1,)),
+    ]
+    work = 6 * chunk * experts * pieces * rows * dim
+    h_par, c_par, part = pl.pallas_call(
+        pair_first_kernel,
+        in_specs=[any_spec, vmem_spec, vmem_spec, any_spec],
+        out_specs=[any_spec, vmem_spec, any_spec],
+        out_shape=[
+            jax.ShapeDtypeStruct(normed.shape, jnp.bfloat16),
+            jax.ShapeDtypeStruct(c_own.shape, jnp.float32),
+            jax.ShapeDtypeStruct((CHUNKS + 1, chunk, dim), jnp.float32),
+        ],
+        scratch_shapes=[
+            pltpu.VMEM((CHUNKS + 1, chunk, dim), jnp.float32), pltpu.VMEM((chunk, c_own.shape[1]), jnp.float32), *bufs,
+            pltpu.SemaphoreType.DMA((2, 2 * CHUNKS)),
+        ],
+        compiler_params=pltpu.CompilerParams(collective_id=cid, has_side_effects=True, vmem_limit_bytes=62 << 20),
+        cost_estimate=pl.CostEstimate(flops=3 * work, bytes_accessed=wa.size * 6, transcendentals=0),
+    )(normed, c_own, c_send, wa)
+    return pl.pallas_call(
+        pair_second_kernel,
+        in_specs=[vmem_spec, any_spec, any_spec, vmem_spec, vmem_spec, any_spec, any_spec, any_spec],
+        out_specs=vmem_spec,
+        out_shape=jax.ShapeDtypeStruct((tokens, dim), jnp.bfloat16),
+        scratch_shapes=[
+            pltpu.VMEM((2 * CHUNKS, chunk, dim), jnp.float32),
+            pltpu.VMEM((CHUNKS, chunk, dim), jnp.float32),
+            *bufs,
+            pltpu.SemaphoreType.DMA((2, CHUNKS)),
+        ],
+        compiler_params=pltpu.CompilerParams(collective_id=cid + 1, has_side_effects=True, vmem_limit_bytes=62 << 20),
+        cost_estimate=pl.CostEstimate(flops=5 * work, bytes_accessed=wa.size * 10, transcendentals=0),
+    )(x, normed, h_par, c_own, c_par, part, wa, other_row)
 
 
 def solution(mesh):
@@ -249,12 +511,35 @@
     def local_program(x, norm_w, router_w, w_gate, w_up, w_down, expert_idx):
         layers = w_gate.shape[0]
         packed = [jnp.stack([w_gate[l].transpose(0, 2, 1), w_up[l].transpose(0, 2, 1), w_down[l]], axis=0) for l in range(layers)]
+        last, me = layers - 1, lax.axis_index("ep")
         gathered = [lax.all_gather(packed[l], "fsdp", axis=0) for l in range(layers)]
+        gathered_mirror = None
         for l in range(layers):
             normed = rms_norm(x, norm_w[l])
             coeff = route_coeffs(normed, router_w[l], expert_idx[l])
-            h_all, c_all = share_tokens(n, normed, coeff.T, 2 * l)
-            x = moe_layer(n, x, normed, h_all, c_all.transpose(0, 2, 1), gathered[l], 2 * l + 1)
+            experts = coeff.shape[1] // n
+            if l < last:
+                h_all, c_all = share_tokens(n, normed, coeff.T, 2 * l)
+                c_all = c_all.transpose(0, 2, 1)
+                far = lax.rem(me + n // 2, n)
+                if l == 0:
+                    h_all, to_send = lax.optimization_barrier((h_all, packed[last]))
+                    mirrored = lax.ppermute(to_send, "ep", [(i, n - 1 - i) for i in range(n)])
+                far_part = block_ffn(
+                    lax.dynamic_index_in_dim(h_all, far, keepdims=False), lax.dynamic_index_in_dim(c_all, far, keepdims=False), gathered[l]
+                )
+                if l == 0:
+                    far_part, mirrored = lax.optimization_barrier((far_part, mirrored))
+                    gathered_mirror = lax.all_gather(mirrored, "fsdp", axis=0)
+                x = moe_layer(n, x, normed, h_all, c_all, gathered[l], far_part, 2 * l + 1)
+            else:
+                peer = me + 1 - 2 * (me % 2)
+
+                def rows_for(who):
+                    cols = [lax.dynamic_slice_in_dim(coeff, row * experts, experts, axis=1) for row in (who, n - 1 - who)]
+                    return jnp.pad(jnp.concatenate(cols, axis=1), ((0, 0), (0, max(0, 128 - 2 * experts))))
+
+                x = pair_layer(x, normed, rows_for(me), rows_for(peer), gathered[l], gathered_mirror, 2 * l)
         return x
 
     return jax.shard_map(local_program, mesh=mesh, in_specs=in_specs, out_specs=tok_spec, check_vma=False)

time: 558 us -> 502 us (0.90)
  Pallas kernels: 481 us -> 426 us
  waiting for transfers between devices: 35.1 us -> 28.6 us
    pallas_call x0 -> x3, Pallas kernels: none -> 205 us  [the longest x1 112 us: pair_layer(): pl.pallas_call(pair_second_kernel, in_specs=[vmem_spec, any_spec, any_spe...]
    pallas_call x2 -> x1, Pallas kernels: 331 us -> 144 us  [moe_layer(): pl.pallas_call(functools.partial(moe_kernel, n), in_specs=[vmem_spec, any...]
    pallas_call x2 -> x1, Pallas kernels: 150 us -> 76.7 us  [share_tokens(): pl.pallas_call(functools.partial(share_kernel, n), in_specs=[pl.BlockSpec...]
    all_gather x2, waiting for transfers between devices: 35 us -> 28.4 us  [local_program(): lax.all_gather(packed[l], 'fsdp', axis=0)]
  transfers between devices with their start and end apart: 2 -> 4, of which waited for: 1 -> 1; matrix products, arithmetic and copies ran while one was open for 3% -> 4% of each run, Pallas kernels for 57% -> 63%
where the time goes in v4:
time: 502 us; the launch traced here: 501 us
  Pallas kernels  426 us (85%)
  waiting for transfers between devices  28.6 us (6%)
  local copies, waits for them, and re-layouts  19.7 us (4%)
  between operations  13.4 us (3%)
  other arithmetic  9.53 us (2%)
    pallas_call x1, Pallas kernels, moe_layer(): pl.pallas_call(functools.partial(moe_kernel, n), in_specs=[vmem_spec, any...  144 us
    pallas_call x1, Pallas kernels, pair_layer(): pl.pallas_call(pair_second_kernel, in_specs=[vmem_spec, any_spec, any_spe...  112 us
    pallas_call x1, Pallas kernels, share_tokens(): pl.pallas_call(functools.partial(share_kernel, n), in_specs=[pl.BlockSpec...  76.7 us
    pallas_call x1, Pallas kernels, pair_layer(): pl.pallas_call(pair_first_kernel, in_specs=[any_spec, vmem_spec, vmem_spe...  60 us
    pallas_call x1, Pallas kernels, block_ffn(): pl.pallas_call(block_kernel, grid=(experts,), in_specs=[pl.BlockSpec((tok...  32.7 us
    all_gather x2, waiting for transfers between devices, local_program(): lax.all_gather(packed[l], 'fsdp', axis=0)  28.4 us
  transfers between devices with their start and end apart: 4, of which 1 were waited for; matrix products, arithmetic and copies ran while one was open for 4% of the time, Pallas kernels for 63%

profile of v4, /device:TPU:97, one launch (start us, length us, event | category | flops | bytes accessed | tf_op | source)
XLA Modules:
  0.0 501.2 jit_solution(16039155675102800837)
XLA Ops:
  6.6 1.9 fusion.20
  8.5 0.3 copy-done.5
  8.8 0.6 copy-done.6
  9.4 0.6 slice_bitcast_fusion
  10.1 2.0 pad_maximum_fusion.1
  12.2 2.0 pad_maximum_fusion
  14.3 0.7 copy-done.10
  15.0 0.9 fusion.6
  15.9 0.5 fusion
  16.4 0.6 fusion.21
  17.0 0.5 fusion.2.h_ref.h_own
  17.6 0.7 select_reduce_fusion.2
  18.4 0.5 copy-done.2
  18.9 0.7 fusion.11.c_ref
  19.6 76.7 %shard_map.73 = (bf16[4,1024,1024]{2,1,0:T(8,128)(2,1)}, f32[4,8,1024]{2,1,0:T(8,128)}) custom-call(bf16[1024,1024]{1,0:T(8,128)(2,1)} %copy-done.2, f32[4,8,1024]{2,1,0:T(8,128)} %fusion.11.c_ref), custom_call_target="tpu_custom_call" | custom-call | flops 60000002048 | bytes 8388608 | tf_op jit(solution)/shard_map/pallas_call | solution.py:76
  96.4 2.2 collective-permute-start
  98.6 2.9 copy.32
  101.4 1.9 dynamic-slice_bitcast_fusion.1.c_ref
  103.3 3.1 dynamic-slice_bitcast_fusion.h_ref
  106.4 28.4 %all-gather.7.cloned.1.call-done = bf16[24,8,64,1024]{3,2,1,0:T(8,128)(2,1)} async-done(((bf16[3,8,64,1024]{3,2,1,0:T(8,128)(2,1)}), bf16[24,8,64,1024]{3,2,1,0:T(8,128)(2,1)}) %all-gather.7.cloned.1.call-update) | async-done | bytes 25165840 | tf_op jit(solution)/shard_map/all_gather | solution.py:515
  134.9 32.7 %shard_map.74.far_hbm = f32[1024,1024]{1,0:T(8,128)} custom-call(bf16[1024,1024]{1,0:T(8,128)(2,1)} %dynamic-slice_bitcast_fusion.h_ref, f32[1024,8]{1,0:T(8,128)} %dynamic-slice_bitcast_fusion.1.c_ref, bf16[8,3,8,64,1024]{4,3,2,1,0:T(8,128)(2,1)} %bitcast.71), custom_call_target="tpu_custom_call" | custom-call | flops 25769803776 | bytes 25165824 | tf_op jit(solution)/shard_map/pallas_call | solution.py:116
  167.6 144.2 %shard_map.75.x_ref = bf16[1024,1024]{1,0:T(8,128)(2,1)} custom-call(bf16[1024,1024]{1,0:T(8,128)(2,1)} %x_ref.1, bf16[1024,1024]{1,0:T(8,128)(2,1)} %copy-done.2, bf16[4,1024,1024]{2,1,0:T(8,128)(2,1)} %get-tuple-element.15.h_all, f32[4,1024,8]{2,1,0:T(8,128)} %bitcast.66, bf16[8,3,8,64,1024]{4,3,2,1,0:T(8,128)(2,1)} %bitcast.72, ...), custom_call_target="tpu_custom_call" | custom-call | flops 77309411328 | bytes 201326592 | tf_op jit(solution)/shard_map/pallas_call | solution.py:262
  311.9 2.2 fusion.3
  314.1 0.5 fusion.5.h_own
  314.7 1.3 copy-done.4
  316.0 0.7 select_reduce_fusion
  317.1 0.2 copy.34
  317.3 0.8 pad.8.c_send
  318.2 0.9 pad.7.c_own
  319.0 60.0 %shard_map.76 = (bf16[1024,1024]{1,0:T(8,128)(2,1)}, f32[1024,128]{1,0:T(8,128)}, f32[3,512,1024]{2,1,0:T(8,128)}) custom-call(bf16[1024,1024]{1,0:T(8,128)(2,1)} %copy-done.4, f32[1024,128]{1,0:T(8,128)} %pad.7.c_own, f32[1024,128]{1,0:T(8,128)} %pad.8.c_send, bf16[8,3,8,64,1024]{4,3,2,1,0:T(8,128)(2,1)} %bitcast.69), custom_call_target="tpu_custom_call" | custom-call | flops 38654705664 | bytes 75497472 | tf_op jit(solution)/shard_map/pallas_call | solution.py:473
  379.1 112.5 %shard_map.77 = bf16[1024,1024]{1,0:T(8,128)(2,1)} custom-call(bf16[1024,1024]{1,0:T(8,128)(2,1)} %shard_map.75.x_ref, bf16[1024,1024]{1,0:T(8,128)(2,1)} %copy-done.4, bf16[1024,1024]{1,0:T(8,128)(2,1)} %get-tuple-element.19.h_par, f32[1024,128]{1,0:T(8,128)} %pad.7.c_own, f32[1024,128]{1,0:T(8,128)} %get-tuple-element.20.c_par, ...), custom_call_target="tpu_custom_call" | custom-call | flops 64424509440 | bytes 125829120 | tf_op jit(solution)/shard_map/pallas_call | solution.py:489
  491.6 3.1 copy.37
  (40 shorter events, 0.8 us)
Async XLA Ops:
  6.5 128.3 %all-gather.7.cloned.1.call-start = ((), (), s32[]{:S(2)}) async-start(), calls=%async_computation | async-start | bytes 28311552 | tf_op jit(solution)/shard_map/all_gather | solution.py:515
  6.6 2.2 copy-start.5
  6.6 2.9 copy-start.6
  12.1 306.9 %all-gather.9.cloned.1.call-start = ((), (), s32[]{:S(2)}) async-start(), calls=%async_computation.1 | async-start | bytes 28311552 | tf_op jit(solution)/shard_map/all_gather | solution.py:515
  14.2 0.8 copy-start.10
  14.2 1.8 copy-start.1
  14.2 2.3 copy-start.12
  14.2 364.8 %all-gather.11.cloned.1.call-start = ((), (), s32[]{:S(2)}) async-start(), calls=%async_computation.2 | async-start | bytes 28311552 | tf_op jit(solution)/shard_map/all_gather | solution.py:533
  15.9 1.7 copy-start.8
  17.6 1.3 copy-start.2
  19.6 76.8 %copy-start = (bf16[3,8,64,1024]{3,2,1,0:T(8,128)(2,1)S(1)}, bf16[3,8,64,1024]{3,2,1,0:T(8,128)(2,1)}, u32[]{:S(2)}) copy-start(bf16[3,8,64,1024]{3,2,1,0:T(8,128)(2,1)} %pad_maximum_fusion) | copy-start | bytes 9437188
  96.4 71.2 %collective-permute-start = (bf16[3,8,64,1024]{3,2,1,0:T(8,128)(2,1)S(1)}, bf16[3,8,64,1024]{3,2,1,0:T(8,128)(2,1)}, u32[]{:S(2)}, u32[]{:S(2)}) collective-permute-start(bf16[3,8,64,1024]{3,2,1,0:T(8,128)(2,1)S(1)} %copy-done), channel_id=1, source_target_pairs={{0,24},{8,16},{16,8},{24,0},{1,25},{9,17},{17,9},{25,1},{2,26},{10... | collective-permute-start | bytes 9437192 | tf_op jit(solution)/shard_map/ppermute | solution.py:527
  167.6 146.5 %copy-start.11 = (f32[1,1024]{1,0:T(1,128)S(1)}, f32[1,1024]{1,0:T(1,128)}, u32[]{:S(2)}) copy-start(f32[1,1024]{1,0:T(1,128)} %get-tuple-element.35) | copy-start | bytes 12292
  311.8 2.3 copy-start.3
  311.8 4.2 copy-start.7
  311.9 4.1 copy-start.9
  314.7 1.3 copy-start.4
Sparse Core Ops, SparseCore 0:
  12.2 122.5 all-gather.6
  136.4 119.1 all-gather.8
  257.2 119.1 all-gather.10
